TPU v7x, 32 devices: a whole 2x2x4 slice. The times are simulated.
32 devices in a mesh: px: 8 (over y, x, core), py: 4 (over z).
Axes of the slice: x: 2, y: 2, z: 4, core: 2. Of those that a mesh axis runs over, the one named last changes fastest.
Arguments:
- cell_ids: int32 [8, 2560, 128], P('px', 'py'), may hold values from 0 to 262143, as said below
- offset_x: bfloat16 [8, 2560, 128], P('px', 'py'), may hold values from 0 to 1
- offset_y: bfloat16 [8, 2560, 128], P('px', 'py'), may hold values from 0 to 1
- mass: bfloat16 [8, 2560, 128], P('px', 'py'), may hold values from 0.25 to 4
- live: int32 [8, 2560, 128], P('px', 'py'), may hold values from 0 to 1, as said below
- tile_owner: int32 [8, 2560], P('px', 'py'), may hold values from 0 to 7, as said below
- counts: int32 [8, 4, 64], P('px', 'py'), may hold values from 0 to 30720, as said below
Outputs:
- spectrum: float32 [2, 8, 1024, 1024], P(None, None, ('px', 'py'))
- bucket_start: int32 [8, 4, 64], P('px', 'py')
Inputs may be any that keep to these rules, and one draw needn't show every extreme that they name: A device's tiles stand in order of bucket, bucket = tile_owner * 8 + plane. One device has at most 240 tiles of one owner; in every draw, in each column of py, one owner has exactly 240 tiles on every device of that column. `cell_ids`: cell = (plane * 128 + row) * 256 + column, with row inside the owner's block of rows and column inside the device's block of columns; all slots of a tile, padded ones too, carry the tile's plane. In a tile the live particles come first; only the last tile of a bucket on a device has padded slots. counts[i, j, b] is the number of live particles in the tiles of bucket b on device (i, j); in every draw some bucket of every device holds 30720.
All inputs are finite; a program needn't handle non-finite values.
Results may differ from a plain program's by a relative error of at most 0.0003.
The roundings to bfloat16 on the way count: a program that leaves them out, or rounds other values in their place, can miss the bound.
Values may be sent and summed in bfloat16 or wider, within the bound.
A program may use at most 192 MiB of HBM per device.

v0:
```python
import functools
import math

import jax
import jax.numpy as jnp
import numpy as np
from jax import lax
from jax.experimental import pallas as pl
from jax.experimental.pallas import tpu as pltpu
from jax.sharding import PartitionSpec as P

NX = 1024
NY = 1024
PLANES = 8
BETA = 18.4
LANES = 128
GROUP = 4


def tap_blocks(start, fraction, scaling):
    rows = lax.broadcasted_iota(jnp.int32, (8, LANES), 0)
    first = jnp.broadcast_to(start, (8, LANES)) - 3
    depth = (rows - first) & 7
    z = ((depth - 3).astype(jnp.float32) - fraction) * 0.25
    taps = jnp.exp(BETA * (jnp.sqrt(jnp.maximum(1.0 - z * z, 0.0)) - 1.0))
    if scaling is not None:
        taps = taps * scaling
    block = (first + depth) >> 3
    odd = (block & 1) == 1
    zero = jnp.zeros_like(taps)
    both = jnp.concatenate(
        [jnp.where(odd, zero, taps), jnp.where(odd, taps, zero)], axis=0
    ).astype(jnp.bfloat16)
    half = block >> 1
    return both, half


def spread_kernel(row_count, col_count, bucket_count, starts_ref, lx_ref, ly_ref, fx_ref, fy_ref,
                  w_ref, out_ref, acc_ref, wx_ref, wy_ref):
    col_blocks = col_count // 16
    lane_tiles = NX // LANES
    out_ref[...] = jnp.zeros_like(out_ref)
    wx_ref[...] = jnp.zeros_like(wx_ref)
    height = col_count + 16
    lane = lax.broadcasted_iota(jnp.int32, (height, LANES), 1)

    def bucket(b, _):
        begin = starts_ref[b]
        end = starts_ref[b + 1]
        chunks = (end - begin + GROUP - 1) // GROUP

        @pl.when(chunks > 0)
        def _():
            acc_ref[...] = jnp.zeros_like(acc_ref)

            def chunk(c, _):
                for g in range(GROUP):
                    t = begin + c * GROUP + g
                    at = pl.ds(t, 1)
                    scale = jnp.where(t < end, 1.0, 0.0)
                    taps, block = tap_blocks(lx_ref[at, :], fx_ref[at, :], None)
                    block = jnp.concatenate([block, block], axis=0).astype(jnp.int16)
                    none = jnp.zeros_like(taps)
                    cols = pl.ds(g * LANES, LANES)
                    for k in range(9):
                        wx_ref[pl.ds(k * 16, 16), cols] = jnp.where(block == k, taps, none)
                    wx_ref[pl.ds(240, 16), cols] = jnp.where(block == -1, taps, none)
                    taps, block = tap_blocks(ly_ref[at, :], fy_ref[at, :], w_ref[at, :] * scale)
                    block = jnp.where(block < 0, col_blocks, block)
                    block = jnp.concatenate([block, block], axis=0).astype(jnp.int16)
                    for k in range(col_blocks + 1):
                        wy_ref[pl.ds(k * 16, 16), cols] = jnp.where(block == k, taps, none)
                acc_ref[...] += lax.dot_general(
                    wy_ref[...], wx_ref[...], (((1,), (1,)), ((), ())),
                    preferred_element_type=jnp.float32,
                )
                return 0

            lax.fori_loop(0, chunks, chunk, 0)
            plane = b % PLANES
            tile = (b // PLANES * row_count) // LANES
            here = pl.ds(pl.multiple_of(tile * LANES, LANES), LANES)
            after = pl.ds(pl.multiple_of((tile + 1) % lane_tiles * LANES, LANES), LANES)
            before = pl.ds(pl.multiple_of((tile + lane_tiles - 1) % lane_tiles * LANES, LANES), LANES)
            out_ref[plane, :, here] += acc_ref[:, :LANES]
            rim = acc_ref[:, LANES:]
            out_ref[plane, :, after] += jnp.where(lane < 64, rim, 0.0)
            out_ref[plane, :, before] += jnp.where(lane < 64, 0.0, rim)
        return 0

    lax.fori_loop(0, bucket_count, bucket, 0)


def spread(starts, lx, ly, fx, fy, w, row_count, col_count):
    height = col_count + 16
    bucket_count = starts.shape[0] - 1
    vmem = pl.BlockSpec(memory_space=pltpu.VMEM)
    return pl.pallas_call(
        functools.partial(spread_kernel, row_count, col_count, bucket_count),
        out_shape=jax.ShapeDtypeStruct((PLANES, height, NX), jnp.float32),
        in_specs=[pl.BlockSpec(memory_space=pltpu.SMEM)] + [vmem] * 5,
        out_specs=vmem,
        scratch_shapes=[
            pltpu.VMEM((height, 2 * LANES), jnp.float32),
            pltpu.VMEM((2 * LANES, GROUP * LANES), jnp.bfloat16),
            pltpu.VMEM((height, GROUP * LANES), jnp.bfloat16),
        ],
        compiler_params=pltpu.CompilerParams(vmem_limit_bytes=40 * 1024 * 1024),
        name="spread",
    )(starts, lx, ly, fx, fy, w)


def split(value):
    high = lax.reduce_precision(value, 8, 7)
    return high.astype(jnp.bfloat16), (value - high).astype(jnp.bfloat16)


def dft_tables():
    n = np.arange(NX)
    k = np.arange(32)
    coarse = 2.0 * np.pi / NX * ((32 * k[:, None] * n[None, :]) % NX)
    fine = 2.0 * np.pi / NX * ((k[:, None] * n[None, :]) % NX)
    cc, cs, fc, fs = lax.optimization_barrier(
        tuple(jnp.asarray(f(a), jnp.float32) for a in (coarse, fine) for f in (np.cos, np.sin))
    )
    cc, cs = cc[:, None, :], cs[:, None, :]
    fc, fs = fc[None, :, :], fs[None, :, :]
    cosine = (cc * fc - cs * fs).reshape(NX, NX)
    sine = (cs * fc + cc * fs).reshape(NX, NX)
    return split(cosine) + split(sine)


def dot(a, b):
    return jnp.dot(a, b, preferred_element_type=jnp.float32)


def power_of(top):
    return jnp.clip(jnp.floor(jnp.log2(jnp.maximum(top, 1e-30))) + 1.0, -90.0, 90.0).astype(jnp.int32)


def scale_of(power):
    return jnp.exp2((power - 15).astype(jnp.float32))


def coded_as(value, power):
    steps = jnp.round(value * jnp.exp2((15 - power).astype(jnp.float32)))
    return jnp.clip(steps, -32767.0, 32767.0).astype(jnp.int16)


def coded_rows(value, spare):
    power = power_of(jnp.max(jnp.abs(value), axis=-2, keepdims=True))
    row = lax.broadcasted_iota(jnp.int32, value.shape, value.ndim - 2)
    return jnp.where(row == spare, power.astype(jnp.int16), coded_as(value, power))


def plain_rows(coded, spare):
    power = lax.slice_in_dim(coded, spare, spare + 1, axis=coded.ndim - 2).astype(jnp.int32)
    row = lax.broadcasted_iota(jnp.int32, coded.shape, coded.ndim - 2)
    return jnp.where(row == spare, 0.0, coded.astype(jnp.float32) * scale_of(power))


def digits(value, width):
    power = power_of(value)
    scaled = value * jnp.exp2((14 - power).astype(jnp.float32))
    high = jnp.clip(jnp.floor(scaled), 0.0, 32767.0)
    low = jnp.clip(jnp.floor((scaled - high) * 16384.0), 0.0, 16384.0)
    lane = lax.broadcasted_iota(jnp.int32, (1, width), 1)
    rest = jnp.where(lane == 1, high, low).astype(jnp.int32)
    return jnp.where(lane == 0, power, rest)


def number(row):
    value = row[..., 1].astype(jnp.float32) + row[..., 2].astype(jnp.float32) / 16384.0
    return value * jnp.exp2((row[..., 0] - 14).astype(jnp.float32))


def local(cell_ids, offset_x, offset_y, mass, live, tile_owner, counts):
    px_count = lax.axis_size("px")
    py_count = lax.axis_size("py")
    row_count = NX // px_count
    col_count = NY // py_count
    parts = px_count // PLANES
    cells = cell_ids[0]
    owners = tile_owner[0]
    buckets = owners * PLANES + cells[:, 0] // (row_count * col_count)
    edges = jnp.arange(px_count * PLANES + 1, dtype=jnp.int32)
    starts = jnp.sum((buckets[None, :] < edges[:, None]).astype(jnp.int32), axis=1)

    def padded(value):
        return jnp.pad(value, ((0, 8), (0, 0)))

    ly = padded(cells % col_count)
    lx = padded((cells // col_count % row_count + owners[:, None] * row_count) % LANES)
    fx = padded(offset_x[0].astype(jnp.float32))
    fy = padded(offset_y[0].astype(jnp.float32))
    w = padded(jnp.where(live[0] == 1, mass[0], jnp.zeros_like(mass[0])).astype(jnp.float32))
    grid = spread(starts, lx, ly, fx, fy, w, row_count, col_count)
    height = col_count + 16
    width = NX // parts
    if parts > 1:
        grid = grid.reshape(PLANES, height, parts, width).transpose(0, 2, 1, 3)
    grid = grid.reshape(px_count // 2, 2, height, width)
    side = lax.axis_index("px") % 2
    keep = lax.dynamic_index_in_dim(grid, side, 1, keepdims=False)
    away = lax.dynamic_index_in_dim(grid, 1 - side, 1, keepdims=False)
    pairs = [(source, source ^ 1) for source in range(px_count)]
    summed = keep + lax.ppermute(away, "px", pairs)
    groups = [list(range(k, px_count, 2)) for k in range(2)]
    got = lax.all_to_all(
        coded_rows(summed, col_count + 8), "px", 0, 0, axis_index_groups=groups, tiled=True
    )
    mine = jnp.sum(plain_rows(got, col_count + 8), axis=0)
    total = jnp.sum(mine)
    by_cols = lax.all_to_all(
        coded_rows(mine, col_count + 8), "py", split_axis=1, concat_axis=0, tiled=True
    )
    part = width // py_count
    ext = plain_rows(by_cols.reshape(py_count, height, part), col_count + 8)
    core = ext[:, :col_count]
    right = jnp.roll(ext[:, col_count : col_count + 4], 1, axis=0)
    left = jnp.roll(ext[:, col_count + 12 :], -1, axis=0)
    core = core + jnp.concatenate(
        [right, jnp.zeros((py_count, col_count - 8, part), jnp.float32), left], axis=1
    )
    data = core.reshape(NY, part)
    cos_hi, cos_lo, sin_hi, sin_lo = dft_tables()
    hi, lo = split(data)
    both = jnp.concatenate([hi, lo], axis=1)
    real = dot(cos_hi, both)
    real = real[:, :part] + real[:, part:] + dot(cos_lo, hi)
    imag = dot(sin_hi, both)
    imag = -(imag[:, :part] + imag[:, part:] + dot(sin_lo, hi))
    devices = px_count * py_count
    ky_part = NY // devices
    lines = jnp.stack([real.reshape(devices, ky_part, part), imag.reshape(devices, ky_part, part)], 1)
    lines = lines.reshape(devices, 2 * ky_part, part)
    power = power_of(jnp.max(jnp.abs(lines), axis=1, keepdims=True))
    coded = coded_as(lines, power)
    bucket_count = counts.shape[-1]
    count_rows = -(-bucket_count // part)
    spare = -(2 + count_rows) % 8
    side_rows = jnp.concatenate(
        [
            digits(total, part),
            jnp.pad(counts.reshape(-1), (0, count_rows * part - bucket_count)).reshape(-1, part),
            jnp.zeros((spare, part), jnp.int32),
        ]
    ).astype(jnp.int16)
    side_rows = jnp.broadcast_to(side_rows[None], (devices,) + side_rows.shape)
    coded = jnp.concatenate([coded, power.astype(jnp.int16), side_rows], axis=1)
    got = lax.all_to_all(coded, ("px", "py"), split_axis=0, concat_axis=0, tiled=True)
    after = got[:, 2 * ky_part :].astype(jnp.int32)
    lines = got[:, : 2 * ky_part].astype(jnp.float32) * scale_of(after[:, :1])
    total = jnp.sum(number(after[:, 1]))
    column = after[:, 2 : 2 + count_rows].reshape(px_count, py_count, 1, count_rows * part)
    column = lax.dynamic_index_in_dim(column, lax.axis_index("py"), 1, keepdims=False)
    column = column[:, :, :bucket_count][:, None]
    got = lines.reshape(PLANES, parts * py_count, 2, ky_part, part).transpose(2, 0, 3, 1, 4)
    got = got.reshape(2 * PLANES * ky_part, NX)
    hi, lo = split(got)
    rows = PLANES * ky_part
    both = jnp.concatenate([hi, lo], axis=0)
    by_cos = dot(both, cos_hi)
    by_cos = by_cos[: 2 * rows] + by_cos[2 * rows :] + dot(hi, cos_lo)
    by_sin = dot(both, sin_hi)
    by_sin = by_sin[: 2 * rows] + by_sin[2 * rows :] + dot(hi, sin_lo)
    out = jnp.stack([by_cos[:rows] + by_sin[rows:], by_cos[rows:] - by_sin[:rows]])
    out = out.reshape(2, PLANES, ky_part, NX)
    norm = 1.0 / math.sqrt(NX * NY)
    index = lax.axis_index("px") * py_count + lax.axis_index("py")
    shape = (2, 1, ky_part, NX)
    at_zero = (
        (lax.broadcasted_iota(jnp.int32, shape, 0) == 0)
        & (lax.broadcasted_iota(jnp.int32, shape, 2) + index == 0)
        & (lax.broadcasted_iota(jnp.int32, shape, 3) == 0)
    )
    spectrum = out * (PLANES * NX * NY * norm / total) - jnp.where(at_zero, NX * NY * norm, 0.0)
    column_sum = jnp.sum(column, axis=0)
    reached = lax.broadcasted_iota(jnp.int32, column.shape, 0) < lax.axis_index("px")
    earlier = jnp.sum(jnp.where(reached, column, 0), axis=0)
    preceding = jnp.cumsum(column_sum, axis=-1) - column_sum
    bucket_start = (preceding + earlier).astype(jnp.int32)
    return (spectrum, bucket_start)


def solution(mesh):
    placed = (
        P("px", "py", None),
        P("px", "py", None),
        P("px", "py", None),
        P("px", "py", None),
        P("px", "py", None),
        P("px", "py"),
        P("px", "py", None),
    )
    return jax.shard_map(
        local,
        mesh=mesh,
        in_specs=placed,
        out_specs=(P(None, None, ("px", "py"), None), P("px", "py", None)),
        check_vma=False,
    )
```

profile of v0, /device:TPU:16, one launch (start us, length us, event | category | flops | bytes accessed | tf_op | source)
XLA Modules:
  0.0 213.5 jit_solution(2302986730504060030)
XLA Ops:
  0.7 1.2 slice_reduce_fusion
  2.6 1.5 add_select_fusion
  4.5 69.0 %spread.1 = f32[8,272,1024]{2,1,0:T(8,128)S(1)} custom-call(s32[65]{0:T(128)S(1)} %convert_reduce_fusion.starts_ref, s32[648,128]{1,0:T(8,128)S(1)} %pad.28.lx_ref, s32[648,128]{1,0:T(8,128)S(1)} %pad.29.ly_ref, f32[648,128]{1,0:T(8,128)S(1)} %pad_convert_fusion.2.fx_ref, f32[648,128]{1,0:T(8,128)S(1)} %get-tuple-element.45.fy_ref, ...), custom_call_target="tpu_custom_call" | custom-call | tf_op jit(solution)/shard_map/spread/pallas_call | solution.py:98
  73.5 3.1 %dynamic-slice_bitcast_fusion = f32[4,272,1024]{2,1,0:T(8,128)} fusion(f32[4,2,272,1024]{3,2,1,0:T(8,128)S(1)} %bitcast.88, s32[]{:T(128)S(6)} %select_n.128), kind=kLoop, calls=%fused_computation.10 | loop fusion | bytes 8912900 | tf_op jit(solution)/shard_map/jit(dynamic_index_in_dim)/squeeze | solution.py:205
  76.6 1.6 copy-done
  78.2 7.9 %collective-permute-done = f32[4,272,1024]{2,1,0:T(8,128)} collective-permute-done((f32[4,272,1024]{2,1,0:T(8,128)}, f32[4,272,1024]{2,1,0:T(8,128)}, u32[]{:S(2)}, u32[]{:S(2)}) %collective-permute-start) | collective-permute-done | bytes 4456480 | tf_op jit(solution)/shard_map/ppermute | solution.py:207
  86.1 4.8 %abs_reduce_fusion = f32[4,1024]{1,0:T(4,128)S(1)} fusion(f32[4,272,1024]{2,1,0:T(8,128)} %collective-permute-done, f32[4,2,272,1024]{3,2,1,0:T(8,128)} %bitcast.89, s32[]{:T(128)S(6)} %select_n.127), kind=kLoop, calls=%fused_computation.9 | loop fusion | flops 3338240 | bytes 8929284 | tf_op jit(solution)/shard_map/reduce_max | solution.py:151
  91.0 1.3 copy-done.1
  92.2 3.5 %fusion.4 = s16[4,272,1024]{2,1,0:T(8,128)(2,1)S(1)} fusion(f32[4,1024]{1,0:T(4,128)S(1)} %get-tuple-element.39, pred[272]{0:T(512)(128)(4,1)S(1)} %iota_compare_fusion.2, f32[4,272,1024]{2,1,0:T(8,128)} %collective-permute-done, f32[4,2,272,1024]{3,2,1,0:T(8,128)S(1)} %bitcast.90, s32[]{:T(128)S(6)} %select_n.127, s16[4,1024]{1,0:T(4,128)(2,1)S(1)} %get-tuple-element.38), kind=kLoop, calls=%fused_computation.17 | loop fusion | flops 6684672 | bytes 11165972 | tf_op jit(solution)/shard_map/jit(_where)/select_n | solution.py:153
  95.8 29.9 %all_to_all.23 = s16[4,272,1024]{2,1,0:T(8,128)(2,1)S(1)} all-to-all(s16[4,272,1024]{2,1,0:T(8,128)(2,1)S(1)} %fusion.4), channel_id=1, replica_groups={{0,8,16,24},{4,12,20,28},{1,9,17,25},{5,13,21,29},{2,10,18,26},{6,14,22..., dimensions={0} | all-to-all | bytes 4456448 | tf_op jit(solution)/shard_map/all_to_all | solution.py:209
  125.8 2.1 %fusion.1 = (f32[272,1024]{1,0:T(8,128)S(1)}, f32[]{:T(128)}) fusion(s16[4,272,1024]{2,1,0:T(8,128)(2,1)S(1)} %all_to_all.23, f32[4,1024]{1,0:T(4,128)S(1)} %bitcast.116, pred[272]{0:T(512)(128)(4,1)S(1)} %iota_compare_fusion.2), kind=kLoop, calls=%fused_computation.7 | loop fusion | flops 5292031 | bytes 3358996 | tf_op jit(solution)/shard_map/reduce_sum | solution.py:212
  128.6 1.0 fusion.19
  129.6 0.9 copy.38
  130.5 5.5 %all-to-all-start.1 = ((s16[272,4,256]{2,0,1:T(8,128)(2,1)}), s16[272,4,256]{2,0,1:T(8,128)(2,1)S(1)}, u32[]{:S(2)}, u32[]{:S(2)}) async-start(s16[272,4,256]{2,0,1:T(8,128)(2,1)} %copy.38), calls=%async_computation.1 | async-start | bytes 1114112 | tf_op jit(solution)/shard_map/all_to_all | solution.py:214
  136.3 3.8 %reduce-precision_convert_fusion.1 = (bf16[32,32,1024]{2,1,0:T(8,128)(2,1)}, bf16[32,32,1024]{2,1,0:T(8,128)(2,1)}, bf16[32,32,1024]{2,1,0:T(8,128)(2,1)S(1)}, bf16[32,32,1024]{2,1,0:T(8,128)(2,1)}) fusion(f32[32,1024]{1,0:T(8,128)S(1)} %copy-done.16, f32[32,1024]{1,0:T(8,128)S(1)} %copy-done.14, f32[32,1024]{1,0:T(8,128)S(1)} %copy-done.15, ...), kind=kLoop, calls=%fused_computation.3 | loop fusion | flops 14680064 | bytes 8912896 | tf_op jit(solution)/shard_map/convert_element_type | solution.py:115
  141.6 5.1 %all-to-all-done.1 = s16[272,4,256]{2,0,1:T(8,128)(2,1)S(1)} async-done(((s16[272,4,256]{2,0,1:T(8,128)(2,1)}), s16[272,4,256]{2,0,1:T(8,128)(2,1)S(1)}, u32[]{:S(2)}, u32[]{:S(2)}) %all-to-all-start.1) | async-done | bytes 557088 | tf_op jit(solution)/shard_map/all_to_all | solution.py:214
  147.3 1.2 copy-done.6
  148.5 1.2 fusion.18
  150.1 1.2 fusion.17
  152.4 0.7 fusion.13
  153.9 1.2 pad_add_fusion
  155.0 5.8 %all-to-all-start.2 = ((s16[32,72,256]{2,1,0:T(8,128)(2,1)}), s16[32,72,256]{2,1,0:T(8,128)(2,1)S(1)}, u32[]{:S(2)}, u32[]{:S(2)}) async-start(s16[32,72,256]{2,1,0:T(8,128)(2,1)} %pad_add_fusion), calls=%async_computation.2 | async-start | bytes 2359296 | tf_op jit(solution)/shard_map/all_to_all | solution.py:251
  161.0 27.1 %all-to-all-done.2 = s16[32,72,256]{2,1,0:T(8,128)(2,1)S(1)} async-done(((s16[32,72,256]{2,1,0:T(8,128)(2,1)}), s16[32,72,256]{2,1,0:T(8,128)(2,1)S(1)}, u32[]{:S(2)}, u32[]{:S(2)}) %all-to-all-start.2) | async-done | bytes 1179680 | tf_op jit(solution)/shard_map/all_to_all | solution.py:251
  189.2 1.4 copy.43
  190.6 1.4 fusion.9
  193.0 1.1 copy-done.7
  194.1 4.3 %fusion.15 = f32[1024,1024]{1,0:T(8,128)} fusion(bf16[1024,1024]{1,0:T(8,128)(2,1)S(1)} %bitcast.110, bf16[512,1024]{1,0:T(8,128)(2,1)S(1)} %get-tuple-element.19, bf16[512,1024]{1,0:T(8,128)(2,1)S(1)} %get-tuple-element.18), kind=kOutput, calls=%fused_computation.41 | convolution fusion | flops 2151677952 | bytes 8388608 | tf_op jit(solution)/shard_map/dot_general | solution.py:134
  198.4 4.3 %fusion.14 = f32[1024,1024]{1,0:T(8,128)} fusion(bf16[1024,1024]{1,0:T(8,128)(2,1)S(1)} %bitcast.108, bf16[512,1024]{1,0:T(8,128)(2,1)S(1)} %get-tuple-element.19, bf16[512,1024]{1,0:T(8,128)(2,1)S(1)} %get-tuple-element.18), kind=kOutput, calls=%fused_computation.40 | convolution fusion | flops 2151677952 | bytes 8388608 | tf_op jit(solution)/shard_map/dot_general | solution.py:134
  203.2 1.4 copy-done.3
  204.6 3.7 %fusion.7 = f32[512,1024]{1,0:T(8,128)S(1)} fusion(f32[1024,1024]{1,0:T(8,128)} %fusion.15, bf16[512,1024]{1,0:T(8,128)(2,1)S(1)} %bitcast.112, bf16[1024,1024]{1,0:T(8,128)(2,1)S(1)} %bitcast.96), kind=kOutput, calls=%fused_computation.22 | convolution fusion | flops 1074790400 | bytes 9437184 | tf_op jit(solution)/shard_map/dot_general | solution.py:134
  208.3 1.3 fusion.6
  212.0 1.6 fusion.8
  (95 shorter events, 9.0 us)
Async XLA Ops:
  0.6 3.7 %copy-start.11 = (bf16[1,640,128]{2,1,0:T(8,128)(2,1)S(1)}, bf16[1,640,128]{2,1,0:T(8,128)(2,1)}, u32[]{:S(2)}) copy-start(bf16[1,640,128]{2,1,0:T(8,128)(2,1)} %param.12) | copy-start | bytes 491524
  0.6 3.7 %copy-start.10 = (bf16[1,640,128]{2,1,0:T(8,128)(2,1)S(1)}, bf16[1,640,128]{2,1,0:T(8,128)(2,1)}, u32[]{:S(2)}) copy-start(bf16[1,640,128]{2,1,0:T(8,128)(2,1)} %param.14) | copy-start | bytes 491524
  0.7 3.7 %copy-start.8 = (s32[1,640,128]{2,1,0:T(8,128)S(1)}, s32[1,640,128]{2,1,0:T(8,128)}, u32[]{:S(2)}) copy-start(s32[1,640,128]{2,1,0:T(8,128)} %param.15) | copy-start | bytes 983044
  0.7 3.8 %copy-start.12 = (bf16[1,640,128]{2,1,0:T(8,128)(2,1)S(1)}, bf16[1,640,128]{2,1,0:T(8,128)(2,1)}, u32[]{:S(2)}) copy-start(bf16[1,640,128]{2,1,0:T(8,128)(2,1)} %param.13) | copy-start | bytes 491524
  73.5 4.8 %copy-start = (f32[8,272,1024]{2,1,0:T(8,128)}, f32[8,272,1024]{2,1,0:T(8,128)S(1)}, u32[]{:S(2)}) copy-start(f32[8,272,1024]{2,1,0:T(8,128)S(1)} %spread.1) | copy-start | bytes 26738692
  78.2 7.9 %collective-permute-start = (f32[4,272,1024]{2,1,0:T(8,128)}, f32[4,272,1024]{2,1,0:T(8,128)}, u32[]{:S(2)}, u32[]{:S(2)}) collective-permute-start(f32[4,272,1024]{2,1,0:T(8,128)} %dynamic-slice_bitcast_fusion), channel_id=1, source_target_pairs={{0,4},{4,0},{8,12},{12,8},{16,20},{20,16},{24,28},{28,24},{1,5},{5... | collective-permute-start | bytes 13369352 | tf_op jit(solution)/shard_map/ppermute | solution.py:207
  86.1 6.1 %copy-start.1 = (f32[8,272,1024]{2,1,0:T(8,128)S(1)}, f32[8,272,1024]{2,1,0:T(8,128)}, u32[]{:S(2)}) copy-start(f32[8,272,1024]{2,1,0:T(8,128)} %copy-done) | copy-start | bytes 26738692
  128.5 7.5 %copy-start.18 = (s32[1,1,64]{2,1,0:T(1,128)S(1)}, s32[1,1,64]{2,1,0:T(1,128)}, u32[]{:S(2)}) copy-start(s32[1,1,64]{2,1,0:T(1,128)} %param.17) | copy-start | bytes 772
  128.5 7.7 %copy-start.13 = (f32[32,1024]{1,0:T(8,128)S(1)}, f32[32,1024]{1,0:T(8,128)}, u32[]{:S(2)}) copy-start(f32[32,1024]{1,0:T(8,128)} %constant.178.clone) | copy-start | bytes 393220
  128.5 7.7 %copy-start.14 = (f32[32,1024]{1,0:T(8,128)S(1)}, f32[32,1024]{1,0:T(8,128)}, u32[]{:S(2)}) copy-start(f32[32,1024]{1,0:T(8,128)} %constant.179.clone) | copy-start | bytes 393220
  128.6 7.7 %copy-start.15 = (f32[32,1024]{1,0:T(8,128)S(1)}, f32[32,1024]{1,0:T(8,128)}, u32[]{:S(2)}) copy-start(f32[32,1024]{1,0:T(8,128)} %constant.180.clone) | copy-start | bytes 393220
  128.6 7.7 %copy-start.16 = (f32[32,1024]{1,0:T(8,128)S(1)}, f32[32,1024]{1,0:T(8,128)}, u32[]{:S(2)}) copy-start(f32[32,1024]{1,0:T(8,128)} %constant.181.clone) | copy-start | bytes 393220
  130.5 16.1 %all-to-all-start.1 = ((s16[272,4,256]{2,0,1:T(8,128)(2,1)}), s16[272,4,256]{2,0,1:T(8,128)(2,1)S(1)}, u32[]{:S(2)}, u32[]{:S(2)}) async-start(s16[272,4,256]{2,0,1:T(8,128)(2,1)} %copy.38), calls=%async_computation.1 | async-start | bytes 1114112 | tf_op jit(solution)/shard_map/all_to_all | solution.py:214
  146.9 1.6 copy-start.6
  148.5 1.6 copy-start.4
  150.1 1.6 copy-start.2
  155.0 33.1 %all-to-all-start.2 = ((s16[32,72,256]{2,1,0:T(8,128)(2,1)}), s16[32,72,256]{2,1,0:T(8,128)(2,1)S(1)}, u32[]{:S(2)}, u32[]{:S(2)}) async-start(s16[32,72,256]{2,1,0:T(8,128)(2,1)} %pad_add_fusion), calls=%async_computation.2 | async-start | bytes 2359296 | tf_op jit(solution)/shard_map/all_to_all | solution.py:251
  192.5 1.6 copy-start.7
  194.1 4.3 %copy-start.5 = (bf16[32,32,1024]{2,1,0:T(8,128)(2,1)S(1)}, bf16[32,32,1024]{2,1,0:T(8,128)(2,1)}, u32[]{:S(2)}) copy-start(bf16[32,32,1024]{2,1,0:T(8,128)(2,1)} %get-tuple-element.29) | copy-start | bytes 6291460
  198.4 4.3 %copy-start.17 = (s32[32,1,256]{2,0,1:T(8,128)S(1)}, s32[32,1,256]{2,0,1:T(8,128)}, u32[]{:S(2)}) copy-start(s32[32,1,256]{2,0,1:T(8,128)} %get-tuple-element.34) | copy-start | bytes 98308
  203.0 1.6 copy-start.3
  204.6 3.7 %copy-start.19 = (f32[1024,1024]{1,0:T(8,128)S(1)}, f32[1024,1024]{1,0:T(8,128)}, u32[]{:S(2)}) copy-start(f32[1024,1024]{1,0:T(8,128)} %fusion.14) | copy-start | bytes 12582916
  208.3 1.3 copy-start.9
where the time goes:
time: 217 us; the launch traced here: 214 us
  Pallas kernels  69 us (32%)
  waiting for transfers between devices  40.1 us (18%)
  blocking collectives  29.9 us (14%)
  other arithmetic  26.4 us (12%)
  matrix products  17.5 us (8%)
  local copies, waits for them, and re-layouts  16.2 us (7%)
  starting transfers between devices  11.3 us (5%)
  between operations  3.27 us (2%)
    pallas_call x1, Pallas kernels, spread(): pl.pallas_call(functools.partial(spread_kernel, row_count, col_count, buc...  69 us
    all_to_all x1, blocking collectives, local(): lax.all_to_all(coded_rows(summed, col_count + 8), 'px', 0, 0, axis_index_...  29.9 us
    all_to_all x1, waiting for transfers between devices, local(): lax.all_to_all(coded, ('px', 'py'), split_axis=0, concat_axis=0, tiled=True)  27.1 us
    dot_general x8, matrix products, dot(): return jnp.dot(a, b, preferred_element_type=jnp.float32)  17.5 us
    unnamed x44, local copies, waits for them, and re-layouts  8.06 us
    ppermute x1, waiting for transfers between devices, local(): summed = keep + lax.ppermute(away, 'px', pairs)  7.87 us
    convert_element_type x5, other arithmetic, split(): return (high.astype(jnp.bfloat16), (value - high).astype(jnp.bfloat16))  6 us
    all_to_all x1, starting transfers between devices, local(): lax.all_to_all(coded, ('px', 'py'), split_axis=0, concat_axis=0, tiled=True)  5.76 us
  transfers between devices with their start and end apart: 3, of which 3 were waited for; matrix products, arithmetic and copies ran while one was open for 2% of the time, Pallas kernels for 0%

commit v1 on v0

v1 whole, which is shorter than its diff:
```python
import functools
import math

import jax
import jax.numpy as jnp
import numpy as np
from jax import lax
from jax.experimental import pallas as pl
from jax.experimental.pallas import tpu as pltpu
from jax.sharding import PartitionSpec as P

NX = 1024
NY = 1024
PLANES = 8
BETA = 18.4
LANES = 128
GROUP = 4
UNROLL = 8
EAGER = 3
RATE = BETA / math.log(2.0)


def tap_blocks(start, fraction, scaling, rows):
    depth = (rows - start + 3) & 7
    z = ((depth - 3).astype(jnp.float32) - fraction) * 0.25
    u = jnp.maximum(1.0 - z * z, 0.0)
    taps = jnp.exp2(u * lax.rsqrt(jnp.maximum(u, 1e-30)) * RATE - RATE)
    if scaling is not None:
        taps = taps * scaling
    at = start - 3 + depth
    odd = (at & 8) != 0
    zero = jnp.zeros_like(taps)
    both = jnp.concatenate(
        [jnp.where(odd, zero, taps), jnp.where(odd, taps, zero)], axis=0
    ).astype(jnp.bfloat16)
    return both, at >> 4


def placed_blocks(taps, block, count):
    block = jnp.where(block < 0, count, block)
    block = jnp.concatenate([block, block], axis=0).astype(jnp.int16)
    none = jnp.zeros_like(taps)
    return [jnp.where(block == k, taps, none) for k in range(count + 1)]


def spread_kernel(row_count, col_count, bucket_count, starts_ref, cell_ref, owner_ref, fx_ref, fy_ref,
                  mass_ref, live_ref, out_ref, rim_ref, x_ref, y_ref, w_ref, c_ref, item_ref):
    tiles = cell_ref.shape[0]
    col_blocks = col_count // 16
    lane_tiles = NX // LANES
    owners_tile = LANES // row_count if row_count < LANES else 1
    height = col_count + 16
    rows = lax.broadcasted_iota(jnp.int32, (8, LANES), 0)
    spare = pl.ds(tiles, 8)
    x_ref[pl.ds(0, tiles), :] = fx_ref[...].astype(jnp.float32)
    y_ref[pl.ds(0, tiles), :] = fy_ref[...].astype(jnp.float32)
    mass = mass_ref[...].astype(jnp.float32)
    w_ref[pl.ds(0, tiles), :] = jnp.where(live_ref[...] == 1, mass, jnp.zeros_like(mass))
    c_ref[pl.ds(0, tiles), :] = cell_ref[...]
    for ref in (x_ref, y_ref, w_ref, c_ref):
        ref[spare, :] = jnp.zeros((8, LANES), ref.dtype)
    out_ref[...] = jnp.zeros_like(out_ref)
    rim_ref[...] = jnp.zeros_like(rim_ref)

    def of_bucket(b, at):
        begin = starts_ref[b]
        count = (starts_ref[b + 1] - begin + GROUP - 1) // GROUP
        word = b * 65536 + begin
        for c in range(EAGER):
            item_ref[at + c] = word + c * GROUP

        @pl.when(count > EAGER)
        def _():
            def one(c, _):
                item_ref[at + c] = word + c * GROUP
                return 0

            lax.fori_loop(EAGER, count, one, 0)

        return at + count

    items = lax.fori_loop(0, bucket_count, of_bucket, 0)
    for k in range(UNROLL):
        item_ref[items + k] = (bucket_count - 1) * 65536 + tiles

    def product(k):
        begin = item_ref[k] & 65535
        bucket = lax.shift_right_logical(item_ref[k], 16)
        end = starts_ref[bucket + 1]
        shift = bucket // PLANES % owners_tile * row_count
        wxs, wys = [], []
        for g in range(GROUP):
            t = begin + g
            at = pl.ds(t, 1)
            scale = jnp.where(t < end, 1.0, 0.0)
            cell = jnp.broadcast_to(c_ref[at, :], (8, LANES))
            lx = lax.shift_right_logical(cell, col_count.bit_length() - 1) & (row_count - 1)
            if owners_tile > 1:
                lx = lx + shift
            taps, block = tap_blocks(lx, x_ref[at, :], None, rows)
            wxs.append(jnp.concatenate(placed_blocks(taps, block, LANES // 16), axis=0))
            taps, block = tap_blocks(cell & (col_count - 1), y_ref[at, :], w_ref[at, :] * scale, rows)
            wys.append(jnp.concatenate(placed_blocks(taps, block, col_blocks), axis=0))
        return lax.dot_general(
            jnp.concatenate(wys, axis=1), jnp.concatenate(wxs, axis=1),
            (((1,), (1,)), ((), ())), preferred_element_type=jnp.float32
        )

    def some(i, _):
        results = [product(i * UNROLL + u) for u in range(UNROLL)]
        for u, result in enumerate(results):
            b = lax.shift_right_logical(item_ref[i * UNROLL + u], 16)
            plane = b % PLANES
            tile = (b // PLANES * row_count) // LANES
            out_ref[plane, tile] += result[:, :LANES]
            rim_ref[plane, tile] += jnp.concatenate(
                [result[:, LANES:], jnp.zeros((height, LANES - 16), jnp.float32)], axis=1
            )
        return 0

    lax.fori_loop(0, (items + UNROLL - 1) // UNROLL, some, 0)

    lane = lax.broadcasted_iota(jnp.int32, (8, LANES), 1)

    def close(i, _):
        plane = i // 2
        for k in range(lane_tiles // 2):
            tile = i % 2 * (lane_tiles // 2) + k
            low = (tile + lane_tiles - 1) % lane_tiles
            high = (tile + 1) % lane_tiles
            for r in range(0, height, 8):
                at = pl.ds(r, 8)
                left = jnp.where(lane < 8, rim_ref[plane, low, at, :], 0.0)
                right = jnp.where(lane < 8, 0.0, rim_ref[plane, high, at, :])
                out_ref[plane, tile, at, :] += left + pltpu.roll(right, LANES - 16, 1)
        return 0

    lax.fori_loop(0, 2 * PLANES, close, 0)


def spread(starts, cells, owners, fx, fy, mass, live, row_count, col_count):
    height = col_count + 16
    bucket_count = starts.shape[0] - 1
    tiles = cells.shape[0]
    vmem = pl.BlockSpec(memory_space=pltpu.VMEM)
    smem = pl.BlockSpec(memory_space=pltpu.SMEM)
    width = LANES + 16
    depth = GROUP * LANES
    return pl.pallas_call(
        functools.partial(spread_kernel, row_count, col_count, bucket_count),
        out_shape=jax.ShapeDtypeStruct((PLANES, NX // LANES, height, LANES), jnp.float32),
        in_specs=[smem, vmem, smem] + [vmem] * 4,
        out_specs=vmem,
        scratch_shapes=[
            pltpu.VMEM((PLANES, NX // LANES, height, LANES), jnp.float32),
            pltpu.VMEM((tiles + 8, LANES), jnp.float32),
            pltpu.VMEM((tiles + 8, LANES), jnp.float32),
            pltpu.VMEM((tiles + 8, LANES), jnp.float32),
            pltpu.VMEM((tiles + 8, LANES), jnp.int32),
            pltpu.SMEM((-(-tiles // GROUP) + bucket_count + UNROLL + EAGER,), jnp.int32),
        ],
        compiler_params=pltpu.CompilerParams(vmem_limit_bytes=40 * 1024 * 1024),
        name="spread",
    )(starts, cells, owners, fx, fy, mass, live)


def split(value):
    high = lax.reduce_precision(value, 8, 7)
    return high.astype(jnp.bfloat16), (value - high).astype(jnp.bfloat16)


def dft_parts():
    n = np.arange(NX)
    k = np.arange(32)
    coarse = 2.0 * np.pi / NX * ((32 * k[:, None] * n[None, :]) % NX)
    fine = 2.0 * np.pi / NX * ((k[:, None] * n[None, :]) % NX)
    return tuple(jnp.asarray(f(a), jnp.float32) for a in (coarse, fine) for f in (np.cos, np.sin))


def dft_tables():
    cc, cs, fc, fs = lax.optimization_barrier(dft_parts())
    cc, cs = cc[:, None, :], cs[:, None, :]
    fc, fs = fc[None, :, :], fs[None, :, :]
    cosine = (cc * fc - cs * fs).reshape(NX, NX)
    sine = (cs * fc + cc * fs).reshape(NX, NX)
    return split(cosine) + split(sine)


def dot(a, b):
    return jnp.dot(a, b, preferred_element_type=jnp.float32)


def power_of(top):
    return jnp.clip(jnp.floor(jnp.log2(jnp.maximum(top, 1e-30))) + 1.0, -90.0, 90.0).astype(jnp.int32)


def scale_of(power):
    return jnp.exp2((power - 15).astype(jnp.float32))


def coded_as(value, power):
    steps = jnp.round(value * jnp.exp2((15 - power).astype(jnp.float32)))
    return jnp.clip(steps, -32767.0, 32767.0).astype(jnp.int16)


def coded_rows(value, spare):
    power = power_of(jnp.max(jnp.abs(value), axis=-2, keepdims=True))
    row = lax.broadcasted_iota(jnp.int32, value.shape, value.ndim - 2)
    return jnp.where(row == spare, power.astype(jnp.int16), coded_as(value, power))


def plain_rows(coded, spare):
    power = lax.slice_in_dim(coded, spare, spare + 1, axis=coded.ndim - 2).astype(jnp.int32)
    row = lax.broadcasted_iota(jnp.int32, coded.shape, coded.ndim - 2)
    return jnp.where(row == spare, 0.0, coded.astype(jnp.float32) * scale_of(power))


def digits(value, width):
    power = power_of(value)
    scaled = value * jnp.exp2((14 - power).astype(jnp.float32))
    high = jnp.clip(jnp.floor(scaled), 0.0, 32767.0)
    low = jnp.clip(jnp.floor((scaled - high) * 16384.0), 0.0, 16384.0)
    lane = lax.broadcasted_iota(jnp.int32, (1, width), 1)
    rest = jnp.where(lane == 1, high, low).astype(jnp.int32)
    return jnp.where(lane == 0, power, rest)


def number(row):
    value = row[..., 1].astype(jnp.float32) + row[..., 2].astype(jnp.float32) / 16384.0
    return value * jnp.exp2((row[..., 0] - 14).astype(jnp.float32))


def scaled(out, total):
    py_count = lax.axis_size("py")
    ky_part = out.shape[2]
    norm = 1.0 / math.sqrt(NX * NY)
    index = lax.axis_index("px") * py_count + lax.axis_index("py")
    shape = (2, 1, ky_part, NX)
    at_zero = (
        (lax.broadcasted_iota(jnp.int32, shape, 0) == 0)
        & (lax.broadcasted_iota(jnp.int32, shape, 2) + index == 0)
        & (lax.broadcasted_iota(jnp.int32, shape, 3) == 0)
    )
    return out * (PLANES * NX * NY * norm / total) - jnp.where(at_zero, NX * NY * norm, 0.0)


def code_power(top):
    return jnp.clip(jnp.floor(jnp.log2(jnp.maximum(top, 1e-30))) + 1.0, -90.0, 90.0)


def code_block(read, store, row_groups, spare):
    top = None
    for r in range(row_groups):
        here = jnp.abs(read(r))
        top = here if top is None else jnp.maximum(top, here)
    power = code_power(jnp.max(top, axis=0, keepdims=True))
    factor = jnp.exp2(15.0 - power)
    for r in range(row_groups):
        steps = jnp.clip(jnp.round(read(r) * factor), -32767.0, 32767.0)
        if r == row_groups - 1 and spare is not None:
            row = lax.broadcasted_iota(jnp.int32, steps.shape, 0)
            steps = jnp.where(row == spare, power, steps)
        store(r, steps.astype(jnp.int32).astype(jnp.int16))
    return power


def exchange_kernel(px_count, py_count, grid_ref, counts_ref, coarse_c_ref, coarse_s_ref, fine_c_ref,
                    fine_s_ref, out_ref, total_ref, starts_ref,
                    pair_ref, own_ref, code_ref, got_ref, zcode_ref, zgot_ref, data_ref, dhl_ref,
                    chi_ref, clo_ref, shi_ref, slo_ref, fcode_ref, fgot_ref, lhs_ref, line_ref,
                    pair_send, pair_recv, code_send, code_recv, z_send, z_recv, f_send, f_recv):
    px = lax.axis_index("px")
    py = lax.axis_index("py")
    core = px % 2
    chip = px // 2
    chips = px_count // 2
    other = px + 1 - 2 * core
    blocks, tiles, height, _ = grid_ref.shape
    part = tiles // py_count
    col_count = height - 16
    groups = height // 16
    spare = 8
    width = part * LANES
    devices = px_count * py_count
    ky_part = NY // devices

    barrier = pltpu.get_barrier_semaphore()
    for e in range(2):
        for s in range(chips):
            for m in range(py_count):
                if e + s + m > 0:
                    to = ((chip + s) % chips * 2 + (core + e) % 2, (py + m) % py_count)
                    pl.semaphore_signal(barrier, inc=1, device_id=to, device_id_type=pl.DeviceIdType.MESH)
    pl.semaphore_wait(barrier, devices - 1)

    order = [(m, s) for m in range(py_count - 1, -1, -1) for s in range(chips - 1, -1, -1)]

    def pair_copy(m, s):
        q = (py + m) % py_count
        block = (chip + s) % chips * 2
        return pltpu.make_async_remote_copy(
            src_ref=grid_ref.at[block + 1 - core, pl.ds(q * part, part)],
            dst_ref=pair_ref.at[m, s],
            send_sem=pair_send.at[m, s],
            recv_sem=pair_recv.at[m, s],
            device_id=(other, py),
            device_id_type=pl.DeviceIdType.MESH,
        )

    def code_copy(m, s):
        return pltpu.make_async_remote_copy(
            src_ref=code_ref.at[m, s],
            dst_ref=got_ref.at[m, s],
            send_sem=code_send.at[m, s],
            recv_sem=code_recv.at[m, s],
            device_id=((chip + s) % chips * 2 + core, py),
            device_id_type=pl.DeviceIdType.MESH,
        )

    def z_copy(m):
        return pltpu.make_async_remote_copy(
            src_ref=zcode_ref.at[m],
            dst_ref=zgot_ref.at[m],
            send_sem=z_send.at[m],
            recv_sem=z_recv.at[m],
            device_id=(px, (py + m) % py_count),
            device_id_type=pl.DeviceIdType.MESH,
        )

    def f_copy(s, e, m):
        return pltpu.make_async_remote_copy(
            src_ref=fcode_ref.at[s, e, m],
            dst_ref=fgot_ref.at[m, s, e],
            send_sem=f_send.at[s, e, m],
            recv_sem=f_recv.at[s, e, m],
            device_id=((chip + s) % chips * 2 + (core + e) % 2, (py + m) % py_count),
            device_id_type=pl.DeviceIdType.MESH,
        )

    for m, s in order:
        pair_copy(m, s).start()

    for m, s in order:
        pair_copy(m, s).wait_recv()
        q = (py + m) % py_count
        block = (chip + s) % chips * 2 + core

        def add(t, _):
            def summed(r):
                at = pl.ds(r * 16, 16)
                return grid_ref[block, q * part + t, at, :] + pair_ref[m, s, t, at, :]

            if s == 0:
                for r in range(groups):
                    own_ref[m, t, pl.ds(r * 16, 16), :] = summed(r)
            else:
                def keep(r, value):
                    code_ref[m, s, t, pl.ds(r * 16, 16), :] = value

                code_block(summed, keep, groups, spare)
            return 0

        lax.fori_loop(0, part, add, 0)
        if s > 0:
            code_copy(m, s).start()

    def table(a, _):
        at = pl.ds(pl.multiple_of(a * 32, 32), 32)
        cc = coarse_c_ref[pl.ds(a, 1), :]
        cs = coarse_s_ref[pl.ds(a, 1), :]
        fc = fine_c_ref[...]
        fs = fine_s_ref[...]
        for value, high_ref, low_ref in (
            (cc * fc - cs * fs, chi_ref, clo_ref),
            (cs * fc + cc * fs, shi_ref, slo_ref),
        ):
            high = value.astype(jnp.bfloat16)
            high_ref[at, :] = high
            low_ref[at, :] = (value - high.astype(jnp.float32)).astype(jnp.bfloat16)
        return 0

    lax.fori_loop(0, NX // 32, table, 0)

    def scale_from(rows):
        return jnp.exp2(rows[8:9].astype(jnp.float32) - 15.0)

    def plain(ref_at, r):
        return ref_at(r).astype(jnp.int32).astype(jnp.float32)

    row16 = lax.broadcasted_iota(jnp.int32, (16, LANES), 0)
    total = jnp.zeros((16, LANES), jnp.float32)
    for m in range(py_count - 1, -1, -1):
        for s in range(chips - 1, 0, -1):
            code_copy(m, s).wait_recv()

        def gather(t, total):
            scales = [
                jnp.exp2(got_ref[m, s, t, pl.ds(col_count, 16), :].astype(jnp.int32)[8:9].astype(jnp.float32) - 15.0)
                for s in range(1, chips)
            ]

            for r in range(groups):
                at = pl.ds(r * 16, 16)
                value = own_ref[m, t, at, :]
                for s in range(1, chips):
                    term = got_ref[m, s, t, at, :].astype(jnp.int32).astype(jnp.float32) * scales[s - 1]
                    if r == groups - 1:
                        term = jnp.where(row16 == spare, 0.0, term)
                    value = value + term
                own_ref[m, t, at, :] = value
                total = total + value
            if m > 0:
                def keep(r, value):
                    zcode_ref[m, t, pl.ds(r * 16, 16), :] = value

                code_block(lambda r: own_ref[m, t, pl.ds(r * 16, 16), :], keep, groups, spare)
            return total

        total = lax.fori_loop(0, part, gather, total)
        if m > 0:
            z_copy(m).start()

    total = jnp.sum(total)

    def place(m, reader):
        source = (py + py_count - m) % py_count
        for t in range(part):
            cols = pl.ds(t * LANES, LANES)
            for r in range(groups - 1):
                data_ref[source, pl.ds(r * 16, 16), cols] = reader(t, r)

    def rims(m, reader):
        source = (py + py_count - m) % py_count
        after = (source + 1) % py_count
        before = (source + py_count - 1) % py_count
        for t in range(part):
            cols = pl.ds(t * LANES, LANES)
            rim = reader(t, groups - 1)
            low = pl.ds(0, 8)
            high = pl.ds(col_count - 8, 8)
            row = lax.broadcasted_iota(jnp.int32, (8, LANES), 0)
            data_ref[after, low, cols] += jnp.where(row < 4, rim[:8], 0.0)
            data_ref[before, high, cols] += jnp.where(row > 4, rim[8:], 0.0)

    def own_reader(t, r):
        return own_ref[0, t, pl.ds(r * 16, 16), :]

    def z_reader(m):
        def read(t, r):
            scale = jnp.exp2(zgot_ref[m, t, pl.ds(col_count, 16), :].astype(jnp.int32)[8:9].astype(jnp.float32) - 15.0)
            return zgot_ref[m, t, pl.ds(r * 16, 16), :].astype(jnp.int32).astype(jnp.float32) * scale
        return read

    readers = [own_reader] + [z_reader(m) for m in range(1, py_count)]
    place(0, readers[0])
    for m in range(py_count - 1, 0, -1):
        z_copy(m).wait_recv()
        place(m, readers[m])
    for m in range(py_count):
        rims(m, readers[m])
    for j in range(py_count):
        def halves(r, _):
            at = pl.ds(pl.multiple_of(r * 16, 16), 16)
            value = data_ref[j, at, :]
            high = value.astype(jnp.bfloat16)
            to = pl.ds(pl.multiple_of(j * col_count + r * 16, 16), 16)
            dhl_ref[0, to, :] = high
            dhl_ref[1, to, :] = (value - high.astype(jnp.float32)).astype(jnp.bfloat16)
            return 0

        lax.fori_loop(0, col_count // 16, halves, 0)

    power = code_power(total)
    scaled = total * jnp.exp2(14.0 - power)
    first = jnp.clip(jnp.floor(scaled), 0.0, 32767.0)
    second = jnp.clip(jnp.floor((scaled - first) * 16384.0), 0.0, 16384.0)
    row8 = lax.broadcasted_iota(jnp.int32, (8, width), 0)
    lane8 = lax.broadcasted_iota(jnp.int32, (8, width), 1)
    number = jnp.where(lane8 == 0, power, jnp.where(lane8 == 1, first, second))
    side = jnp.where(row8 == 1, number, counts_ref[...].astype(jnp.float32))
    span = 2 * py_count * ky_part

    def transform(s):
        at = pl.ds(pl.multiple_of((chip + s) % chips * span, span), span)
        for high_ref, low_ref, k in ((chi_ref, clo_ref, 0), (shi_ref, slo_ref, 1)):
            value = jnp.dot(high_ref[at, :], dhl_ref[0], preferred_element_type=jnp.float32)
            value += jnp.dot(high_ref[at, :], dhl_ref[1], preferred_element_type=jnp.float32)
            value += jnp.dot(low_ref[at, :], dhl_ref[0], preferred_element_type=jnp.float32)
            line_ref[k] = value if k == 0 else -value
        for e in range(2):
            for m in range(py_count):
                index = (core + e) % 2 * py_count + (py + m) % py_count
                rows = pl.ds(pl.multiple_of(index * ky_part, ky_part), ky_part)
                real = line_ref[0, rows, :]
                imag = line_ref[1, rows, :]
                top = jnp.maximum(jnp.abs(real), jnp.abs(imag))
                power = code_power(jnp.max(top, axis=0, keepdims=True))
                factor = jnp.exp2(15.0 - power)
                for k, value in enumerate((real, imag)):
                    steps = jnp.clip(jnp.round(value * factor), -32767.0, 32767.0)
                    fcode_ref[s, e, m, pl.ds(k * ky_part, ky_part), :] = steps.astype(jnp.int32).astype(jnp.int16)
                rest = jnp.where(row8 == 0, power, side)
                fcode_ref[s, e, m, pl.ds(2 * ky_part, 8), :] = rest.astype(jnp.int32).astype(jnp.int16)

    def send_all(s):
        transform(s)
        for e in range(2):
            for m in range(py_count - 1, -1, -1):
                f_copy(s, e, m).start()
        return 0

    lax.fori_loop(0, chips - 1, lambda k, _: send_all(chips - 1 - k), 0)
    transform(0)
    for e in range(1, -1, -1):
        for m in range(py_count - 1, -1, -1):
            if e + m > 0:
                f_copy(0, e, m).start()

    sum_total = total
    column = jnp.zeros((8, width), jnp.float32)
    before = jnp.zeros((8, width), jnp.float32)
    rows_all = px_count * ky_part
    for m in range(py_count):
        source = (py + py_count - m) % py_count
        for s in range(chips):
            for e in range(2):
                mine = m + s + e == 0
                if not mine:
                    f_copy(s, e, m).wait_recv()
                got = fcode_ref if mine else fgot_ref
                where = (0, 0, 0) if mine else (m, s, e)
                sender = (chip + chips - s) % chips * 2 + (core + e) % 2
                rest = got[where + (pl.ds(2 * ky_part, 8), slice(None))].astype(jnp.int32)
                scale = jnp.exp2(rest[0:1].astype(jnp.float32) - 15.0)
                info = rest.astype(jnp.float32)
                if not mine:
                    digit = info[1:2, :LANES]
                    lane1 = lax.broadcasted_iota(jnp.int32, (1, LANES), 1)
                    body = jnp.sum(jnp.where(lane1 == 1, digit, 0.0) + jnp.where(lane1 == 2, digit * (1.0 / 16384.0), 0.0))
                    bits = jnp.sum(jnp.where(lane1 == 0, digit, 0.0))
                    sum_total = sum_total + body * jnp.exp2(bits - 14.0)
                if m == 0:
                    column = column + info
                    before = before + jnp.where(sender < px, info, 0.0)
                rows = pl.ds(pl.multiple_of(sender * ky_part, ky_part), ky_part)
                rows2 = pl.ds(pl.multiple_of(rows_all + sender * ky_part, ky_part), ky_part)
                real = got[where + (pl.ds(0, ky_part), slice(None))].astype(jnp.int32).astype(jnp.float32) * scale
                imag = got[where + (pl.ds(ky_part, ky_part), slice(None))].astype(jnp.int32).astype(jnp.float32) * scale
                for at, a, b in ((rows, real, imag), (rows2, imag, -real)):
                    for k, value in enumerate((a, b)):
                        high = value.astype(jnp.bfloat16)
                        lhs_ref[0, at, pl.ds(k * width, width)] = high
                        lhs_ref[1, at, pl.ds(k * width, width)] = (value - high.astype(jnp.float32)).astype(jnp.bfloat16)

        xrows = pl.ds(pl.multiple_of(source * width, width), width)

        def columns(n, _):
            cols = pl.ds(pl.multiple_of(n * 256, 256), 256)
            high = lhs_ref[0]
            low = lhs_ref[1]
            ch, cl, sh, sl = (ref[xrows, cols] for ref in (chi_ref, clo_ref, shi_ref, slo_ref))
            hh = jnp.concatenate([ch, sh], axis=0)
            ll = jnp.concatenate([cl, sl], axis=0)
            value = jnp.dot(high, hh, preferred_element_type=jnp.float32)
            value += jnp.dot(low, hh, preferred_element_type=jnp.float32)
            value += jnp.dot(high, ll, preferred_element_type=jnp.float32)
            if m == 0:
                out_ref[:, cols] = value
            else:
                out_ref[:, cols] += value
            return 0

        lax.fori_loop(0, NX // 256, columns, 0)

    total_ref[...] = jnp.full((8, LANES), sum_total, jnp.float32)
    sums = column[2:3]
    lane = lax.broadcasted_iota(jnp.int32, (1, width), 1)
    preceding = sums
    step = 1
    while step < width:
        preceding = preceding + jnp.where(lane >= step, pltpu.roll(preceding, step, 1), 0.0)
        step *= 2
    starts_ref[...] = jnp.broadcast_to(preceding - sums + before[2:3], (8, width)).astype(jnp.int32)

    for m, s in order:
        pair_copy(m, s).wait_send()
        if s > 0:
            code_copy(m, s).wait_send()
    for m in range(1, py_count):
        z_copy(m).wait_send()
    for s in range(chips):
        for e in range(2):
            for m in range(py_count):
                if s + e + m > 0:
                    f_copy(s, e, m).wait_send()


def exchange(grid, counts_row, tables, px_count, py_count):
    blocks, tiles, height, _ = grid.shape
    chips = px_count // 2
    part = tiles // py_count
    width = part * LANES
    col_count = height - 16
    ky_part = NY // (px_count * py_count)
    span = 2 * py_count * ky_part
    rows = px_count * ky_part
    vmem = pl.BlockSpec(memory_space=pltpu.VMEM)
    dma = pltpu.SemaphoreType.DMA
    f32, bf16, s16 = jnp.float32, jnp.bfloat16, jnp.int16
    return pl.pallas_call(
        functools.partial(exchange_kernel, px_count, py_count),
        out_shape=(
            jax.ShapeDtypeStruct((2 * rows, NX), f32),
            jax.ShapeDtypeStruct((8, LANES), f32),
            jax.ShapeDtypeStruct((8, width), jnp.int32),
        ),
        in_specs=[vmem] * 6,
        out_specs=[vmem] * 3,
        scratch_shapes=[
            pltpu.VMEM((py_count, chips, part, height, LANES), f32),
            pltpu.VMEM((py_count, part, height, LANES), f32),
            pltpu.VMEM((py_count, chips, part, height, LANES), s16),
            pltpu.VMEM((py_count, chips, part, height, LANES), s16),
            pltpu.VMEM((py_count, part, height, LANES), s16),
            pltpu.VMEM((py_count, part, height, LANES), s16),
            pltpu.VMEM((py_count, col_count, width), f32),
            pltpu.VMEM((2, NY, width), bf16),
        ]
        + [pltpu.VMEM((NX, NX), bf16)] * 4
        + [
            pltpu.VMEM((chips, 2, py_count, 2 * ky_part + 8, width), s16),
            pltpu.VMEM((py_count, chips, 2, 2 * ky_part + 8, width), s16),
            pltpu.VMEM((2, 2 * rows, 2 * width), bf16),
            pltpu.VMEM((2, span, width), f32),
            dma((py_count, chips)),
            dma((py_count, chips)),
            dma((py_count, chips)),
            dma((py_count, chips)),
            dma((py_count,)),
            dma((py_count,)),
            dma((chips, 2, py_count)),
            dma((chips, 2, py_count)),
        ],
        compiler_params=pltpu.CompilerParams(
            collective_id=0, has_side_effects=True, vmem_limit_bytes=62 * 1024 * 1024
        ),
        name="exchange",
    )(grid, counts_row, *tables)


def local(cell_ids, offset_x, offset_y, mass, live, tile_owner, counts):
    px_count = lax.axis_size("px")
    py_count = lax.axis_size("py")
    row_count = NX // px_count
    col_count = NY // py_count
    parts = px_count // PLANES
    cells = cell_ids[0]
    owners = tile_owner[0]
    devices = px_count * py_count
    ky_part = NY // devices
    buckets = owners * PLANES + cells[:, 0] // (row_count * col_count)
    edges = jnp.arange(px_count * PLANES + 1, dtype=jnp.int32)
    starts = jnp.sum((buckets[None, :] < edges[:, None]).astype(jnp.int32), axis=1)

    grid = spread(
        starts, cells, owners, offset_x[0], offset_y[0], mass[0], live[0], row_count, col_count
    )
    bucket_count = counts.shape[-1]
    lane_tiles = NX // LANES
    if px_count == PLANES and lane_tiles % py_count == 0 and bucket_count <= LANES:
        width = lane_tiles // py_count * LANES
        counts_row = jnp.pad(counts.reshape(1, -1), ((2, 5), (0, width - bucket_count)))
        out, total, begin = exchange(grid, counts_row, dft_parts(), px_count, py_count)
        out = out.reshape(2, PLANES, ky_part, NX)
        spectrum = scaled(out, total[0, 0])
        return (spectrum, begin[:1, :bucket_count][None])
    grid = grid.transpose(0, 2, 1, 3).reshape(PLANES, col_count + 16, NX)
    height = col_count + 16
    width = NX // parts
    if parts > 1:
        grid = grid.reshape(PLANES, height, parts, width).transpose(0, 2, 1, 3)
    grid = grid.reshape(px_count // 2, 2, height, width)
    side = lax.axis_index("px") % 2
    keep = lax.dynamic_index_in_dim(grid, side, 1, keepdims=False)
    away = lax.dynamic_index_in_dim(grid, 1 - side, 1, keepdims=False)
    pairs = [(source, source ^ 1) for source in range(px_count)]
    summed = keep + lax.ppermute(away, "px", pairs)
    groups = [list(range(k, px_count, 2)) for k in range(2)]
    got = lax.all_to_all(
        coded_rows(summed, col_count + 8), "px", 0, 0, axis_index_groups=groups, tiled=True
    )
    mine = jnp.sum(plain_rows(got, col_count + 8), axis=0)
    total = jnp.sum(mine)
    by_cols = lax.all_to_all(
        coded_rows(mine, col_count + 8), "py", split_axis=1, concat_axis=0, tiled=True
    )
    part = width // py_count
    ext = plain_rows(by_cols.reshape(py_count, height, part), col_count + 8)
    core = ext[:, :col_count]
    right = jnp.roll(ext[:, col_count : col_count + 4], 1, axis=0)
    left = jnp.roll(ext[:, col_count + 12 :], -1, axis=0)
    core = core + jnp.concatenate(
        [right, jnp.zeros((py_count, col_count - 8, part), jnp.float32), left], axis=1
    )
    data = core.reshape(NY, part)
    cos_hi, cos_lo, sin_hi, sin_lo = dft_tables()
    hi, lo = split(data)
    both = jnp.concatenate([hi, lo], axis=1)
    real = dot(cos_hi, both)
    real = real[:, :part] + real[:, part:] + dot(cos_lo, hi)
    imag = dot(sin_hi, both)
    imag = -(imag[:, :part] + imag[:, part:] + dot(sin_lo, hi))
    lines = jnp.stack([real.reshape(devices, ky_part, part), imag.reshape(devices, ky_part, part)], 1)
    lines = lines.reshape(devices, 2 * ky_part, part)
    power = power_of(jnp.max(jnp.abs(lines), axis=1, keepdims=True))
    coded = coded_as(lines, power)
    count_rows = -(-bucket_count // part)
    spare = -(2 + count_rows) % 8
    side_rows = jnp.concatenate(
        [
            digits(total, part),
            jnp.pad(counts.reshape(-1), (0, count_rows * part - bucket_count)).reshape(-1, part),
            jnp.zeros((spare, part), jnp.int32),
        ]
    ).astype(jnp.int16)
    side_rows = jnp.broadcast_to(side_rows[None], (devices,) + side_rows.shape)
    coded = jnp.concatenate([coded, power.astype(jnp.int16), side_rows], axis=1)
    got = lax.all_to_all(coded, ("px", "py"), split_axis=0, concat_axis=0, tiled=True)
    after = got[:, 2 * ky_part :].astype(jnp.int32)
    lines = got[:, : 2 * ky_part].astype(jnp.float32) * scale_of(after[:, :1])
    total = jnp.sum(number(after[:, 1]))
    column = after[:, 2 : 2 + count_rows].reshape(px_count, py_count, 1, count_rows * part)
    column = lax.dynamic_index_in_dim(column, lax.axis_index("py"), 1, keepdims=False)
    column = column[:, :, :bucket_count][:, None]
    got = lines.reshape(PLANES, parts * py_count, 2, ky_part, part).transpose(2, 0, 3, 1, 4)
    got = got.reshape(2 * PLANES * ky_part, NX)
    hi, lo = split(got)
    rows = PLANES * ky_part
    both = jnp.concatenate([hi, lo], axis=0)
    by_cos = dot(both, cos_hi)
    by_cos = by_cos[: 2 * rows] + by_cos[2 * rows :] + dot(hi, cos_lo)
    by_sin = dot(both, sin_hi)
    by_sin = by_sin[: 2 * rows] + by_sin[2 * rows :] + dot(hi, sin_lo)
    out = jnp.stack([by_cos[:rows] + by_sin[rows:], by_cos[rows:] - by_sin[:rows]])
    out = out.reshape(2, PLANES, ky_part, NX)
    spectrum = scaled(out, total)
    column_sum = jnp.sum(column, axis=0)
    reached = lax.broadcasted_iota(jnp.int32, column.shape, 0) < lax.axis_index("px")
    earlier = jnp.sum(jnp.where(reached, column, 0), axis=0)
    preceding = jnp.cumsum(column_sum, axis=-1) - column_sum
    bucket_start = (preceding + earlier).astype(jnp.int32)
    return (spectrum, bucket_start)


def solution(mesh):
    placed = (
        P("px", "py", None),
        P("px", "py", None),
        P("px", "py", None),
        P("px", "py", None),
        P("px", "py", None),
        P("px", "py"),
        P("px", "py", None),
    )
    return jax.shard_map(
        local,
        mesh=mesh,
        in_specs=placed,
        out_specs=(P(None, None, ("px", "py"), None), P("px", "py", None)),
        check_vma=False,
    )
```

time: 217 us -> 123 us (0.57); the launches traced: 214 us -> 122 us
  waiting for transfers between devices: 40.1 us -> 0 us
  Pallas kernels: 69 us -> 104 us
  blocking collectives: 29.9 us -> 0 us
  other arithmetic: 26.4 us -> 4.24 us
  matrix products: 17.5 us -> 0 us
  starting transfers between devices: 11.3 us -> 0 us
  local copies, waits for them, and re-layouts: 16.2 us -> 12.2 us
    pallas_call x0 -> x1, Pallas kernels: none -> 78.3 us  [exchange(): pl.pallas_call(functools.partial(exchange_kernel, px_count, py_count), ou...]
    pallas_call x1, Pallas kernels: 69 us -> 25.9 us  [spread(): pl.pallas_call(functools.partial(spread_kernel, row_count, col_count, buc...]
    all_to_all x2 -> x0, waiting for transfers between devices: 32.2 us -> none  [the longest x1 27.1 us: local(): lax.all_to_all(coded, ('px', 'py'), split_axis=0, concat_axis=0, tiled=True)]
    all_to_all x1 -> x0, blocking collectives: 29.9 us -> none  [local(): lax.all_to_all(coded_rows(summed, col_count + 8), 'px', 0, 0, axis_index_...]
    dot_general x8 -> x0, matrix products: 17.5 us -> none  [dot(): return jnp.dot(a, b, preferred_element_type=jnp.float32)]
    all_to_all x2 -> x0, starting transfers between devices: 11.3 us -> none  [the longest x1 5.76 us: local(): lax.all_to_all(coded, ('px', 'py'), split_axis=0, concat_axis=0, tiled=True)]
    ppermute x1 -> x0, waiting for transfers between devices: 7.87 us -> none  [local(): summed = keep + lax.ppermute(away, 'px', pairs)]
    convert_element_type x10 -> x0, other arithmetic: 6.46 us -> none  [the longest x5 6 us: split(): return (high.astype(jnp.bfloat16), (value - high).astype(jnp.bfloat16))]
  transfers between devices with their start and end apart: 3 -> 0, of which waited for: 3 -> 0; matrix products, arithmetic and copies ran while one was open for 2% -> 0% of each run, Pallas kernels for 0% -> 0%
where the time goes in v1:
time: 123 us; the launch traced here: 122 us
  Pallas kernels  104 us (85%)
  local copies, waits for them, and re-layouts  12.2 us (10%)
  other arithmetic  4.24 us (3%)
  between operations  1.4 us (1%)
    pallas_call x1, Pallas kernels, exchange(): pl.pallas_call(functools.partial(exchange_kernel, px_count, py_count), ou...  78.3 us
    pallas_call x1, Pallas kernels, spread(): pl.pallas_call(functools.partial(spread_kernel, row_count, col_count, buc...  25.9 us
    unnamed x14, local copies, waits for them, and re-layouts  8.11 us

profile of v1, /device:TPU:16, one launch (start us, length us, event | category | flops | bytes accessed | tf_op | source)
XLA Modules:
  0.0 122.1 jit_solution(12078660565000086697)
XLA Ops:
  0.6 1.1 slice_reduce_fusion
  1.8 0.7 fusion
  2.5 0.1 convert_reduce_fusion.starts_ref
  2.6 0.0 copy-start.1
  2.6 1.0 copy-done.1
  3.6 0.0 copy-start.2
  3.6 1.0 copy-done.2
  4.6 0.0 copy-start.3
  4.6 0.9 copy-done.3
  5.5 0.0 copy-start.4
  5.5 0.9 copy-done.4
  6.4 0.0 copy-start.5
  6.4 0.9 copy-done.5
  7.3 0.0 copy-start.6
  7.3 25.9 %spread.1.grid_ref = f32[8,8,272,128]{3,2,1,0:T(8,128)S(1)} custom-call(s32[65]{0:T(128)S(1)} %convert_reduce_fusion.starts_ref, s32[640,128]{1,0:T(8,128)S(1)} %bitcast.11, s32[640]{0:T(1024)S(1)} %get-tuple-element.8.owner_ref, bf16[640,128]{1,0:T(8,128)(2,1)S(1)} %bitcast.13, bf16[640,128]{1,0:T(8,128)(2,1)S(1)} %bitcast.14, ...), custom_call_target="tpu_custom_call" | custom-call | tf_op jit(solution)/shard_map/spread/pallas_call | solution.py:149
  33.2 0.0 copy-start
  33.2 3.4 %copy-done = f32[8,8,272,128]{3,2,1,0:T(8,128)} copy-done((f32[8,8,272,128]{3,2,1,0:T(8,128)}, f32[8,8,272,128]{3,2,1,0:T(8,128)S(1)}, u32[]{:S(2)}) %copy-start) | copy-done | bytes 8912920
  36.7 0.0 copy-done.6
  36.7 0.6 pad.4.counts_ref
  37.3 78.3 %exchange.1 = (f32[512,1024]{1,0:T(8,128)}, f32[8,128]{1,0:T(8,128)}, s32[8,256]{1,0:T(8,128)}) custom-call(f32[8,8,272,128]{3,2,1,0:T(8,128)} %copy-done, s32[8,256]{1,0:T(8,128)} %pad.4.counts_ref, f32[32,1024]{1,0:T(8,128)} %constant.46.clone.coarse_c_ref, f32[32,1024]{1,0:T(8,128)} %constant.47.clone.coarse_s_ref, f32[32,1024]{1,0:T(8,128)} %constant.48.clone.fine_c_ref, ...), custom_call_target="tpu_custom_call" | custom-call | tf_op jit(solution)/shard_map/exchange/pallas_call | solution.py:610
  115.6 1.2 slice.10
  117.5 1.8 %broadcast_multiply_fusion = f32[512,1024]{1,0:T(8,128)S(1)} fusion(f32[512,1024]{1,0:T(8,128)} %get-tuple-element.5, f32[]{:T(128)} %bitcast.6), kind=kLoop, calls=%fused_computation.1 | loop fusion | flops 524288 | bytes 4194308 | tf_op jit(solution)/shard_map/mul | solution.py:244
  119.3 0.1 and_select_fusion
  119.4 1.5 %broadcast_subtract_fusion = f32[2,8,32,1024]{3,2,1,0:T(8,128)} fusion(f32[2,8,32,1024]{3,2,1,0:T(8,128)S(1)} %bitcast.16, f32[2,32,1024]{2,1,0:T(8,128)S(1)} %and_select_fusion), kind=kLoop, calls=%fused_computation | loop fusion | flops 524288 | bytes 4456448 | tf_op jit(solution)/shard_map/sub | solution.py:244
  120.9 1.2 slice_bitcast_fusion
  (3 shorter events, 0.0 us)
Async XLA Ops:
  2.6 1.0 copy-start.1
  3.6 1.0 copy-start.2
  4.6 0.9 copy-start.3
  5.5 0.9 copy-start.4
  6.4 0.9 copy-start.5
  7.3 29.3 %copy-start.6 = (s32[1,1,64]{2,1,0:T(1,128)S(1)}, s32[1,1,64]{2,1,0:T(1,128)}, u32[]{:S(2)}) copy-start(s32[1,1,64]{2,1,0:T(1,128)} %param.17) | copy-start | bytes 772
  33.2 3.4 %copy-start = (f32[8,8,272,128]{3,2,1,0:T(8,128)}, f32[8,8,272,128]{3,2,1,0:T(8,128)S(1)}, u32[]{:S(2)}) copy-start(f32[8,8,272,128]{3,2,1,0:T(8,128)S(1)} %spread.1.grid_ref) | copy-start | bytes 26738692

commit v2 on v1

--- a/solution.py
+++ b/solution.py
@@ -17,6 +17,8 @@
 GROUP = 4
 UNROLL = 8
 EAGER = 3
+SPREAD_VMEM = 24
+EXCHANGE_VMEM = 34
 RATE = BETA / math.log(2.0)
 
 
@@ -43,28 +45,69 @@
     return [jnp.where(block == k, taps, none) for k in range(count + 1)]
 
 
-def spread_kernel(row_count, col_count, bucket_count, starts_ref, cell_ref, owner_ref, fx_ref, fy_ref,
-                  mass_ref, live_ref, out_ref, rim_ref, x_ref, y_ref, w_ref, c_ref, item_ref):
-    tiles = cell_ref.shape[0]
+def spread_kernel(row_count, col_count, bucket_count, cell_in, owner_in, fx_in, fy_in, mass_in, live_in,
+                  out_ref, rim_ref, owner_ref, x_ref, y_ref, w_ref, c_ref, fx_ref, fy_ref, mass_ref, live_ref,
+                  edge_ref, starts_ref, item_ref, sems, edge_sem):
+    tiles = cell_in.shape[0]
     col_blocks = col_count // 16
     lane_tiles = NX // LANES
     owners_tile = LANES // row_count if row_count < LANES else 1
     height = col_count + 16
     rows = lax.broadcasted_iota(jnp.int32, (8, LANES), 0)
     spare = pl.ds(tiles, 8)
+    copies = [
+        pltpu.make_async_copy(source, target, sems.at[k])
+        for k, (source, target) in enumerate(
+            (
+                (cell_in, c_ref.at[pl.ds(0, tiles)]),
+                (owner_in, owner_ref),
+                (fx_in, fx_ref),
+                (fy_in, fy_ref),
+                (mass_in, mass_ref),
+                (live_in, live_ref),
+            )
+        )
+    ]
+    for copy in copies:
+        copy.start()
+    for ref in (x_ref, y_ref, w_ref, c_ref):
+        ref[spare, :] = jnp.zeros((8, LANES), ref.dtype)
+    rim_ref[...] = jnp.zeros_like(rim_ref)
+
+    copies[0].wait()
+    copies[1].wait()
+    plane_bits = (row_count * col_count).bit_length() - 1
+    groups = edge_ref.shape[0]
+    for g in range(groups):
+        edge = lax.broadcasted_iota(jnp.int32, (LANES, LANES), 1) + g * LANES
+        found = jnp.zeros((8, LANES), jnp.int32)
+        for k in range(0, tiles, LANES):
+            count = min(LANES, tiles - k)
+            owner = jnp.broadcast_to(owner_ref[:, pl.ds(k, LANES)], (LANES, LANES)).T
+            bucket = owner[:count] * PLANES + lax.shift_right_logical(
+                c_ref[pl.ds(k, count), :], plane_bits
+            )
+            lower = jnp.where(bucket < edge[:count], 1, 0)
+            for r in range(0, count, 8):
+                found = found + lower[r : r + 8]
+        edge_ref[pl.ds(g, 1), :] = jnp.sum(found, axis=0, keepdims=True)
+    edges = pltpu.make_async_copy(edge_ref, starts_ref, edge_sem)
+    edges.start()
+    out_ref[...] = jnp.zeros_like(out_ref)
+    for copy in copies[2:]:
+        copy.wait()
     x_ref[pl.ds(0, tiles), :] = fx_ref[...].astype(jnp.float32)
     y_ref[pl.ds(0, tiles), :] = fy_ref[...].astype(jnp.float32)
     mass = mass_ref[...].astype(jnp.float32)
     w_ref[pl.ds(0, tiles), :] = jnp.where(live_ref[...] == 1, mass, jnp.zeros_like(mass))
-    c_ref[pl.ds(0, tiles), :] = cell_ref[...]
-    for ref in (x_ref, y_ref, w_ref, c_ref):
-        ref[spare, :] = jnp.zeros((8, LANES), ref.dtype)
-    out_ref[...] = jnp.zeros_like(out_ref)
-    rim_ref[...] = jnp.zeros_like(rim_ref)
+    edges.wait()
+
+    def start_of(b):
+        return starts_ref[lax.shift_right_logical(b, 7), b & (LANES - 1)]
 
     def of_bucket(b, at):
-        begin = starts_ref[b]
-        count = (starts_ref[b + 1] - begin + GROUP - 1) // GROUP
+        begin = start_of(b)
+        count = (start_of(b + 1) - begin + GROUP - 1) // GROUP
         word = b * 65536 + begin
         for c in range(EAGER):
             item_ref[at + c] = word + c * GROUP
@@ -86,7 +129,7 @@
     def product(k):
         begin = item_ref[k] & 65535
         bucket = lax.shift_right_logical(item_ref[k], 16)
-        end = starts_ref[bucket + 1]
+        end = start_of(bucket + 1)
         shift = bucket // PLANES % owners_tile * row_count
         wxs, wys = [], []
         for g in range(GROUP):
@@ -138,30 +181,39 @@
     lax.fori_loop(0, 2 * PLANES, close, 0)
 
 
-def spread(starts, cells, owners, fx, fy, mass, live, row_count, col_count):
+def spread(cells, owners, fx, fy, mass, live, row_count, col_count, bucket_count):
     height = col_count + 16
-    bucket_count = starts.shape[0] - 1
     tiles = cells.shape[0]
     vmem = pl.BlockSpec(memory_space=pltpu.VMEM)
-    smem = pl.BlockSpec(memory_space=pltpu.SMEM)
-    width = LANES + 16
-    depth = GROUP * LANES
+    anywhere = pl.BlockSpec(memory_space=pltpu.HBM)
+    wide = -(-tiles // LANES) * LANES
+    owners = jnp.pad(owners, ((0, 0), (0, wide - tiles)))
+    edges = (-(-(bucket_count + 1) // LANES), LANES)
     return pl.pallas_call(
         functools.partial(spread_kernel, row_count, col_count, bucket_count),
         out_shape=jax.ShapeDtypeStruct((PLANES, NX // LANES, height, LANES), jnp.float32),
-        in_specs=[smem, vmem, smem] + [vmem] * 4,
+        in_specs=[anywhere] * 6,
         out_specs=vmem,
         scratch_shapes=[
             pltpu.VMEM((PLANES, NX // LANES, height, LANES), jnp.float32),
+            pltpu.VMEM((1, wide), jnp.int32),
             pltpu.VMEM((tiles + 8, LANES), jnp.float32),
             pltpu.VMEM((tiles + 8, LANES), jnp.float32),
             pltpu.VMEM((tiles + 8, LANES), jnp.float32),
             pltpu.VMEM((tiles + 8, LANES), jnp.int32),
+            pltpu.VMEM((tiles, LANES), fx.dtype),
+            pltpu.VMEM((tiles, LANES), fy.dtype),
+            pltpu.VMEM((tiles, LANES), mass.dtype),
+            pltpu.VMEM((tiles, LANES), live.dtype),
+            pltpu.VMEM(edges, jnp.int32),
+            pltpu.SMEM(edges, jnp.int32),
             pltpu.SMEM((-(-tiles // GROUP) + bucket_count + UNROLL + EAGER,), jnp.int32),
+            pltpu.SemaphoreType.DMA((6,)),
+            pltpu.SemaphoreType.DMA,
         ],
-        compiler_params=pltpu.CompilerParams(vmem_limit_bytes=40 * 1024 * 1024),
+        compiler_params=pltpu.CompilerParams(vmem_limit_bytes=SPREAD_VMEM * 1024 * 1024),
         name="spread",
-    )(starts, cells, owners, fx, fy, mass, live)
+    )(*(pltpu.with_memory_space_constraint(v, pltpu.HBM) for v in (cells, owners, fx, fy, mass, live)))
 
 
 def split(value):
@@ -264,8 +316,9 @@
     return power
 
 
-def exchange_kernel(px_count, py_count, grid_ref, counts_ref, coarse_c_ref, coarse_s_ref, fine_c_ref,
-                    fine_s_ref, out_ref, total_ref, starts_ref,
+def exchange_kernel(px_count, py_count, grid_ref, counts_ref, coarse_c_in, coarse_s_in, fine_c_in,
+                    fine_s_in, out_ref, starts_ref,
+                    coarse_c_ref, coarse_s_ref, fine_c_ref, fine_s_ref, side_ref, table_sems,
                     pair_ref, own_ref, code_ref, got_ref, zcode_ref, zgot_ref, data_ref, dhl_ref,
                     chi_ref, clo_ref, shi_ref, slo_ref, fcode_ref, fgot_ref, lhs_ref, line_ref,
                     pair_send, pair_recv, code_send, code_recv, z_send, z_recv, f_send, f_recv):
@@ -284,6 +337,19 @@
     devices = px_count * py_count
     ky_part = NY // devices
 
+    tables = [
+        pltpu.make_async_copy(source, target, table_sems.at[k])
+        for k, (source, target) in enumerate(
+            (
+                (coarse_c_in, coarse_c_ref),
+                (coarse_s_in, coarse_s_ref),
+                (fine_c_in, fine_c_ref),
+                (fine_s_in, fine_s_ref),
+            )
+        )
+    ]
+    for copy in tables:
+        copy.start()
     barrier = pltpu.get_barrier_semaphore()
     for e in range(2):
         for s in range(chips):
@@ -364,6 +430,8 @@
         if s > 0:
             code_copy(m, s).start()
 
+    for copy in tables:
+        copy.wait()
     def table(a, _):
         at = pl.ds(pl.multiple_of(a * 32, 32), 32)
         cc = coarse_c_ref[pl.ds(a, 1), :]
@@ -477,7 +545,10 @@
     row8 = lax.broadcasted_iota(jnp.int32, (8, width), 0)
     lane8 = lax.broadcasted_iota(jnp.int32, (8, width), 1)
     number = jnp.where(lane8 == 0, power, jnp.where(lane8 == 1, first, second))
-    side = jnp.where(row8 == 1, number, counts_ref[...].astype(jnp.float32))
+    bucket_count = counts_ref.shape[1]
+    side_ref[...] = jnp.where(row8 == 1, number, 0.0)
+    side_ref[pl.ds(2, 1), pl.ds(0, bucket_count)] = counts_ref[...].astype(jnp.float32)
+    side = side_ref[...]
     span = 2 * py_count * ky_part
 
     def transform(s):
@@ -552,6 +623,8 @@
                         lhs_ref[0, at, pl.ds(k * width, width)] = high
                         lhs_ref[1, at, pl.ds(k * width, width)] = (value - high.astype(jnp.float32)).astype(jnp.bfloat16)
 
+        norm = 1.0 / math.sqrt(NX * NY)
+        factor = (PLANES * NX * NY * norm) / jnp.full((1, 256), sum_total, jnp.float32)
         xrows = pl.ds(pl.multiple_of(source * width, width), width)
 
         def columns(n, _):
@@ -564,15 +637,20 @@
             value = jnp.dot(high, hh, preferred_element_type=jnp.float32)
             value += jnp.dot(low, hh, preferred_element_type=jnp.float32)
             value += jnp.dot(high, ll, preferred_element_type=jnp.float32)
-            if m == 0:
-                out_ref[:, cols] = value
-            else:
-                out_ref[:, cols] += value
+            if m > 0:
+                value += out_ref[:, cols]
+            if m == py_count - 1:
+                value = value * factor
+            out_ref[:, cols] = value
             return 0
 
         lax.fori_loop(0, NX // 256, columns, 0)
 
-    total_ref[...] = jnp.full((8, LANES), sum_total, jnp.float32)
+    first8 = lax.broadcasted_iota(jnp.int32, (8, LANES), 0) == 0
+    corner = first8 & (lax.broadcasted_iota(jnp.int32, (8, LANES), 1) + px + py == 0)
+    for plane in range(px_count):
+        at = pl.ds(plane * ky_part, 8)
+        out_ref[at, pl.ds(0, LANES)] -= jnp.where(corner, NX * NY * norm, 0.0)
     sums = column[2:3]
     lane = lax.broadcasted_iota(jnp.int32, (1, width), 1)
     preceding = sums
@@ -580,7 +658,8 @@
     while step < width:
         preceding = preceding + jnp.where(lane >= step, pltpu.roll(preceding, step, 1), 0.0)
         step *= 2
-    starts_ref[...] = jnp.broadcast_to(preceding - sums + before[2:3], (8, width)).astype(jnp.int32)
+    begin = (preceding - sums + before[2:3]).astype(jnp.int32)
+    starts_ref[0] = begin[:, :bucket_count]
 
     for m, s in order:
         pair_copy(m, s).wait_send()
@@ -595,7 +674,7 @@
                     f_copy(s, e, m).wait_send()
 
 
-def exchange(grid, counts_row, tables, px_count, py_count):
+def exchange(grid, counts, tables, px_count, py_count):
     blocks, tiles, height, _ = grid.shape
     chips = px_count // 2
     part = tiles // py_count
@@ -611,12 +690,14 @@
         functools.partial(exchange_kernel, px_count, py_count),
         out_shape=(
             jax.ShapeDtypeStruct((2 * rows, NX), f32),
-            jax.ShapeDtypeStruct((8, LANES), f32),
-            jax.ShapeDtypeStruct((8, width), jnp.int32),
+            jax.ShapeDtypeStruct((1,) + counts.shape, jnp.int32),
         ),
-        in_specs=[vmem] * 6,
-        out_specs=[vmem] * 3,
-        scratch_shapes=[
+        in_specs=[vmem] * 2 + [pl.BlockSpec(memory_space=pltpu.HBM)] * 4,
+        out_specs=[vmem] * 2,
+        scratch_shapes=[pltpu.VMEM((32, NX), f32)] * 4
+        + [
+            pltpu.VMEM((8, width), f32),
+            dma((4,)),
             pltpu.VMEM((py_count, chips, part, height, LANES), f32),
             pltpu.VMEM((py_count, part, height, LANES), f32),
             pltpu.VMEM((py_count, chips, part, height, LANES), s16),
@@ -642,10 +723,10 @@
             dma((chips, 2, py_count)),
         ],
         compiler_params=pltpu.CompilerParams(
-            collective_id=0, has_side_effects=True, vmem_limit_bytes=62 * 1024 * 1024
+            collective_id=0, has_side_effects=True, vmem_limit_bytes=EXCHANGE_VMEM * 1024 * 1024
         ),
         name="exchange",
-    )(grid, counts_row, *tables)
+    )(grid, counts, *tables)
 
 
 def local(cell_ids, offset_x, offset_y, mass, live, tile_owner, counts):
@@ -654,26 +735,17 @@
     row_count = NX // px_count
     col_count = NY // py_count
     parts = px_count // PLANES
-    cells = cell_ids[0]
-    owners = tile_owner[0]
     devices = px_count * py_count
     ky_part = NY // devices
-    buckets = owners * PLANES + cells[:, 0] // (row_count * col_count)
-    edges = jnp.arange(px_count * PLANES + 1, dtype=jnp.int32)
-    starts = jnp.sum((buckets[None, :] < edges[:, None]).astype(jnp.int32), axis=1)
-
     grid = spread(
-        starts, cells, owners, offset_x[0], offset_y[0], mass[0], live[0], row_count, col_count
+        cell_ids[0], tile_owner, offset_x[0], offset_y[0], mass[0], live[0], row_count, col_count,
+        px_count * PLANES,
     )
     bucket_count = counts.shape[-1]
     lane_tiles = NX // LANES
     if px_count == PLANES and lane_tiles % py_count == 0 and bucket_count <= LANES:
-        width = lane_tiles // py_count * LANES
-        counts_row = jnp.pad(counts.reshape(1, -1), ((2, 5), (0, width - bucket_count)))
-        out, total, begin = exchange(grid, counts_row, dft_parts(), px_count, py_count)
-        out = out.reshape(2, PLANES, ky_part, NX)
-        spectrum = scaled(out, total[0, 0])
-        return (spectrum, begin[:1, :bucket_count][None])
+        out, begin = exchange(grid, counts[0], dft_parts(), px_count, py_count)
+        return (out.reshape(2, PLANES, ky_part, NX), begin)
     grid = grid.transpose(0, 2, 1, 3).reshape(PLANES, col_count + 16, NX)
     height = col_count + 16
     width = NX // parts

time: 123 us -> 103 us (0.84)
  local copies, waits for them, and re-layouts: 12.2 us -> 1.86 us
  other arithmetic: 4.24 us -> 0 us
  Pallas kernels: 104 us -> 100 us
    unnamed x14 -> x12, local copies, waits for them, and re-layouts: 8.11 us -> 1.86 us
    pallas_call x1, Pallas kernels: 78.3 us -> 73.7 us  [exchange(): pl.pallas_call(functools.partial(exchange_kernel, px_count, py_count), ou...]
    slice x2 -> x0, local copies, waits for them, and re-layouts: 2.34 us -> none  [the longest x1 1.19 us: local(): spectrum = scaled(out, total[0, 0])]
    mul x1 -> x0, other arithmetic: 1.75 us -> none  [scaled(): out * (PLANES * NX * NY * norm / total)]
    sub x1 -> x0, other arithmetic: 1.54 us -> none  [scaled(): out * (PLANES * NX * NY * norm / total)]
where the time goes in v2:
time: 103 us
  Pallas kernels  100 us (97%)
  local copies, waits for them, and re-layouts  1.86 us (2%)
    pallas_call x1, Pallas kernels, exchange(): pl.pallas_call(functools.partial(exchange_kernel, px_count, py_count), ou...  73.7 us
    pallas_call x1, Pallas kernels, spread(): pl.pallas_call(functools.partial(spread_kernel, row_count, col_count, buc...  26.7 us

profile of v2, /device:TPU:16, one launch (start us, length us, event | category | flops | bytes accessed | tf_op | source)
XLA Modules:
  0.0 102.9 jit_solution(13357616909001189861)
XLA Ops:
  0.6 0.0 copy-start
  0.6 0.0 copy-start.1
  0.7 0.0 copy-start.2
  0.7 0.0 copy-start.3
  0.7 0.0 copy-start.4
  0.7 26.7 %spread.1.grid_ref = f32[8,8,272,128]{3,2,1,0:T(8,128)S(1)} custom-call(s32[640,128]{1,0:T(8,128)} %bitcast.9, s32[1,640]{1,0:T(1,128)} %owner_in.1, bf16[640,128]{1,0:T(8,128)(2,1)} %bitcast.11, bf16[640,128]{1,0:T(8,128)(2,1)} %bitcast.12, bf16[640,128]{1,0:T(8,128)(2,1)} %bitcast.13, s32[640,128]{1,0:T(8,128)} %bitcast.10), custom_call_target="tpu_custom_call" | custom-call | tf_op jit(solution)/shard_map/spread/pallas_call | solution.py:192
  27.4 0.0 copy-done
  27.4 0.0 copy-done.1
  27.4 0.0 copy-done.2
  27.4 0.0 copy-done.3
  27.4 0.0 copy-done.4
  27.4 73.7 %exchange.1 = (f32[512,1024]{1,0:T(8,128)S(1)}, s32[1,1,64]{2,1,0:T(1,128)S(1)}) custom-call(f32[8,8,272,128]{3,2,1,0:T(8,128)S(1)} %spread.1.grid_ref, s32[1,64]{1,0:T(1,128)S(1)} %bitcast.8, f32[32,1024]{1,0:T(8,128)S(1)} %copy-done.3, f32[32,1024]{1,0:T(8,128)S(1)} %copy-done.2, f32[32,1024]{1,0:T(8,128)S(1)} %copy-done.1, f32[32,1024]{1,0:T(8,128)S(1)} %copy-done), custom_call_target="tpu_custom_call" | custom-call | tf_op jit(solution)/shard_map/exchange/pallas_call | solution.py:689
  101.1 1.3 %copy.15 = f32[2,8,32,1024]{3,2,1,0:T(8,128)} copy(f32[2,8,32,1024]{3,2,1,0:T(8,128)S(1)} %bitcast.7) | data formatting | bytes 4194304
  102.4 0.5 copy.16
Async XLA Ops:
  0.6 26.7 %copy-start = (f32[32,1024]{1,0:T(8,128)S(1)}, f32[32,1024]{1,0:T(8,128)}, u32[]{:S(2)}) copy-start(f32[32,1024]{1,0:T(8,128)} %constant.12.clone.fine_s_in) | copy-start | bytes 393220
  0.6 26.7 %copy-start.1 = (f32[32,1024]{1,0:T(8,128)S(1)}, f32[32,1024]{1,0:T(8,128)}, u32[]{:S(2)}) copy-start(f32[32,1024]{1,0:T(8,128)} %constant.11.clone.fine_c_in) | copy-start | bytes 393220
  0.7 26.7 %copy-start.2 = (f32[32,1024]{1,0:T(8,128)S(1)}, f32[32,1024]{1,0:T(8,128)}, u32[]{:S(2)}) copy-start(f32[32,1024]{1,0:T(8,128)} %constant.10.clone.coarse_s_in) | copy-start | bytes 393220
  0.7 26.7 %copy-start.3 = (f32[32,1024]{1,0:T(8,128)S(1)}, f32[32,1024]{1,0:T(8,128)}, u32[]{:S(2)}) copy-start(f32[32,1024]{1,0:T(8,128)} %constant.4.clone.coarse_c_in) | copy-start | bytes 393220
  0.7 26.7 %copy-start.4 = (s32[1,1,64]{2,1,0:T(1,128)S(1)}, s32[1,1,64]{2,1,0:T(1,128)}, u32[]{:S(2)}) copy-start(s32[1,1,64]{2,1,0:T(1,128)} %param.17) | copy-start | bytes 772

commit v3 on v2

--- a/solution.py
+++ b/solution.py
@@ -18,7 +18,10 @@
 UNROLL = 8
 EAGER = 3
 SPREAD_VMEM = 24
-EXCHANGE_VMEM = 34
+EXCHANGE_VMEM = 38
+WIDE = 256
+SENDS = (3, 2, 1, 0)
+TAKES = (3, 0, 1, 2)
 RATE = BETA / math.log(2.0)
 
 
@@ -317,11 +320,13 @@
 
 
 def exchange_kernel(px_count, py_count, grid_ref, counts_ref, coarse_c_in, coarse_s_in, fine_c_in,
-                    fine_s_in, out_ref, starts_ref,
-                    coarse_c_ref, coarse_s_ref, fine_c_ref, fine_s_ref, side_ref, table_sems,
-                    pair_ref, own_ref, code_ref, got_ref, zcode_ref, zgot_ref, data_ref, dhl_ref,
+                    fine_s_in, out_ref, starts_ref, factor_ref,
+                    coarse_c_ref, coarse_s_ref, fine_c_ref, fine_s_ref, table_sems,
+                    pair_ref, own_ref, code_ref, got_ref, zcode_ref, zgot_ref, edge_ref, dhl_ref,
                     chi_ref, clo_ref, shi_ref, slo_ref, fcode_ref, fgot_ref, lhs_ref, line_ref,
-                    pair_send, pair_recv, code_send, code_recv, z_send, z_recv, f_send, f_recv):
+                    info_ref, infos_ref,
+                    pair_send, pair_recv, code_send, code_recv, z_send, z_recv, f_send, f_recv,
+                    i_send, i_recv):
     px = lax.axis_index("px")
     py = lax.axis_index("py")
     core = px % 2
@@ -329,13 +334,19 @@
     chips = px_count // 2
     other = px + 1 - 2 * core
     blocks, tiles, height, _ = grid_ref.shape
-    part = tiles // py_count
+    near = py_count // 2
+    half = py // near
+    seat = py % near
+    part = tiles // near
+    chunks = near * part
     col_count = height - 16
     groups = height // 16
     spare = 8
     width = part * LANES
     devices = px_count * py_count
     ky_part = NY // devices
+    norm = 1.0 / math.sqrt(NX * NY)
+    mesh_id = pl.DeviceIdType.MESH
 
     tables = [
         pltpu.make_async_copy(source, target, table_sems.at[k])
@@ -356,332 +367,361 @@
             for m in range(py_count):
                 if e + s + m > 0:
                     to = ((chip + s) % chips * 2 + (core + e) % 2, (py + m) % py_count)
-                    pl.semaphore_signal(barrier, inc=1, device_id=to, device_id_type=pl.DeviceIdType.MESH)
+                    pl.semaphore_signal(barrier, inc=1, device_id=to, device_id_type=mesh_id)
     pl.semaphore_wait(barrier, devices - 1)
 
-    order = [(m, s) for m in range(py_count - 1, -1, -1) for s in range(chips - 1, -1, -1)]
-
-    def pair_copy(m, s):
-        q = (py + m) % py_count
+    def split_of(c):
+        return near - 1 - c // part, c % part
+
+    def tile_of(c):
+        a, k = split_of(c)
+        return (seat + a) % near * part + k
+
+    def pair_copy(c, s):
         block = (chip + s) % chips * 2
         return pltpu.make_async_remote_copy(
-            src_ref=grid_ref.at[block + 1 - core, pl.ds(q * part, part)],
-            dst_ref=pair_ref.at[m, s],
-            send_sem=pair_send.at[m, s],
-            recv_sem=pair_recv.at[m, s],
+            src_ref=grid_ref.at[block + 1 - core, tile_of(c)],
+            dst_ref=pair_ref.at[c, s],
+            send_sem=pair_send.at[c, s],
+            recv_sem=pair_recv.at[c, s],
             device_id=(other, py),
-            device_id_type=pl.DeviceIdType.MESH,
+            device_id_type=mesh_id,
         )
 
-    def code_copy(m, s):
+    def code_copy(c, s):
         return pltpu.make_async_remote_copy(
-            src_ref=code_ref.at[m, s],
-            dst_ref=got_ref.at[m, s],
-            send_sem=code_send.at[m, s],
-            recv_sem=code_recv.at[m, s],
+            src_ref=code_ref.at[c, s - 1],
+            dst_ref=got_ref.at[c, s - 1],
+            send_sem=code_send.at[c, s - 1],
+            recv_sem=code_recv.at[c, s - 1],
             device_id=((chip + s) % chips * 2 + core, py),
-            device_id_type=pl.DeviceIdType.MESH,
+            device_id_type=mesh_id,
         )
 
-    def z_copy(m):
+    def z_copy(a, k, b):
         return pltpu.make_async_remote_copy(
-            src_ref=zcode_ref.at[m],
-            dst_ref=zgot_ref.at[m],
-            send_sem=z_send.at[m],
-            recv_sem=z_recv.at[m],
-            device_id=(px, (py + m) % py_count),
-            device_id_type=pl.DeviceIdType.MESH,
+            src_ref=zcode_ref.at[a, k],
+            dst_ref=zgot_ref.at[a, b, k],
+            send_sem=z_send.at[a, b, k],
+            recv_sem=z_recv.at[a, b, k],
+            device_id=(px, (half + b) % 2 * near + (seat + a) % near),
+            device_id_type=mesh_id,
         )
 
-    def f_copy(s, e, m):
+    def peer(s, e, a):
+        return ((chip + s) % chips * 2 + (core + e) % 2, half * near + (seat + a) % near)
+
+    def f_copy(s, e, a):
         return pltpu.make_async_remote_copy(
-            src_ref=fcode_ref.at[s, e, m],
-            dst_ref=fgot_ref.at[m, s, e],
-            send_sem=f_send.at[s, e, m],
-            recv_sem=f_recv.at[s, e, m],
-            device_id=((chip + s) % chips * 2 + (core + e) % 2, (py + m) % py_count),
-            device_id_type=pl.DeviceIdType.MESH,
+            src_ref=fcode_ref.at[s, e, a],
+            dst_ref=fgot_ref.at[s, e, a],
+            send_sem=f_send.at[s, e, a],
+            recv_sem=f_recv.at[s, e, a],
+            device_id=peer(s, e, a),
+            device_id_type=mesh_id,
         )
 
-    for m, s in order:
-        pair_copy(m, s).start()
-
-    for m, s in order:
-        pair_copy(m, s).wait_recv()
-        q = (py + m) % py_count
-        block = (chip + s) % chips * 2 + core
-
-        def add(t, _):
+    def i_copy(s, e, a):
+        return pltpu.make_async_remote_copy(
+            src_ref=info_ref,
+            dst_ref=infos_ref.at[s, e, a],
+            send_sem=i_send.at[s, e, a],
+            recv_sem=i_recv.at[s, e, a],
+            device_id=peer(s, e, a),
+            device_id_type=mesh_id,
+        )
+
+    others = [(s, e, a) for s in range(chips) for e in range(2) for a in range(near) if s + e + a > 0]
+    moves = [(a, b) for a in range(near - 1, -1, -1) for b in (1, 0) if a + b > 0]
+
+    for c in range(chunks):
+        for s in range(chips - 1, -1, -1):
+            pair_copy(c, s).start()
+
+    def add_pair(c):
+        tile = tile_of(c)
+        for s in range(chips - 1, -1, -1):
+            pair_copy(c, s).wait_recv()
+            block = (chip + s) % chips * 2 + core
+
             def summed(r):
                 at = pl.ds(r * 16, 16)
-                return grid_ref[block, q * part + t, at, :] + pair_ref[m, s, t, at, :]
+                return grid_ref[block, tile, at, :] + pair_ref[c, s, at, :]
 
             if s == 0:
                 for r in range(groups):
-                    own_ref[m, t, pl.ds(r * 16, 16), :] = summed(r)
+                    own_ref[c, pl.ds(r * 16, 16), :] = summed(r)
             else:
                 def keep(r, value):
-                    code_ref[m, s, t, pl.ds(r * 16, 16), :] = value
+                    code_ref[c, s - 1, pl.ds(r * 16, 16), :] = value
 
                 code_block(summed, keep, groups, spare)
+                code_copy(c, s).start()
+
+    def scale_in(rows):
+        return jnp.exp2(rows.astype(jnp.int32)[spare : spare + 1].astype(jnp.float32) - 15.0)
+
+    def plain(rows):
+        return rows.astype(jnp.int32).astype(jnp.float32)
+
+    row16 = lax.broadcasted_iota(jnp.int32, (16, LANES), 0)
+
+    def gather(c):
+        a, k = split_of(c)
+        for s in range(chips - 1, 0, -1):
+            code_copy(c, s).wait_recv()
+        scales = [scale_in(got_ref[c, s, pl.ds(col_count, 16), :]) for s in range(chips - 1)]
+        for r in range(groups):
+            at = pl.ds(r * 16, 16)
+            value = own_ref[c, at, :]
+            for s in range(chips - 1):
+                term = plain(got_ref[c, s, at, :]) * scales[s]
+                if r == groups - 1:
+                    term = jnp.where(row16 == spare, 0.0, term)
+                value = value + term
+            own_ref[c, at, :] = value
+
+        def keep(r, value):
+            zcode_ref[a, k, pl.ds(r * 16, 16), :] = value
+
+        code_block(lambda r: own_ref[c, pl.ds(r * 16, 16), :], keep, groups, spare)
+        for a2, b in moves:
+            if a2 == a:
+                z_copy(a, k, b).start()
+
+    def make_tables():
+        for copy in tables:
+            copy.wait()
+
+        def table(i, _):
+            at = pl.ds(pl.multiple_of(i * 32, 32), 32)
+            cc = coarse_c_ref[pl.ds(i, 1), :]
+            cs = coarse_s_ref[pl.ds(i, 1), :]
+            fc = fine_c_ref[...]
+            fs = fine_s_ref[...]
+            for value, high_ref, low_ref in (
+                (cc * fc - cs * fs, chi_ref, clo_ref),
+                (cs * fc + cc * fs, shi_ref, slo_ref),
+            ):
+                high = value.astype(jnp.bfloat16)
+                high_ref[at, :] = high
+                low_ref[at, :] = (value - high.astype(jnp.float32)).astype(jnp.bfloat16)
             return 0
 
-        lax.fori_loop(0, part, add, 0)
-        if s > 0:
-            code_copy(m, s).start()
-
-    for copy in tables:
-        copy.wait()
-    def table(a, _):
-        at = pl.ds(pl.multiple_of(a * 32, 32), 32)
-        cc = coarse_c_ref[pl.ds(a, 1), :]
-        cs = coarse_s_ref[pl.ds(a, 1), :]
-        fc = fine_c_ref[...]
-        fs = fine_s_ref[...]
-        for value, high_ref, low_ref in (
-            (cc * fc - cs * fs, chi_ref, clo_ref),
-            (cs * fc + cc * fs, shi_ref, slo_ref),
-        ):
-            high = value.astype(jnp.bfloat16)
-            high_ref[at, :] = high
-            low_ref[at, :] = (value - high.astype(jnp.float32)).astype(jnp.bfloat16)
-        return 0
-
-    lax.fori_loop(0, NX // 32, table, 0)
-
-    def scale_from(rows):
-        return jnp.exp2(rows[8:9].astype(jnp.float32) - 15.0)
-
-    def plain(ref_at, r):
-        return ref_at(r).astype(jnp.int32).astype(jnp.float32)
-
-    row16 = lax.broadcasted_iota(jnp.int32, (16, LANES), 0)
+        lax.fori_loop(0, NX // 32, table, 0)
+
+    row8 = lax.broadcasted_iota(jnp.int32, (8, LANES), 0)
+
+    def source_of(a, b):
+        return (half + b) % 2 * near + (seat + near - a) % near
+
+    def rows_in(a, b, k):
+        if a + b == 0:
+            return lambda r: own_ref[(near - 1) * part + k, pl.ds(r * 16, 16), :]
+        scale = scale_in(zgot_ref[a, b, k, pl.ds(col_count, 16), :])
+        return lambda r: plain(zgot_ref[a, b, k, pl.ds(r * 16, 16), :]) * scale
+
+    def put_halves(row, cols, value):
+        at = pl.ds(pl.multiple_of(row, 16), 16)
+        high = value.astype(jnp.bfloat16)
+        dhl_ref[0, at, cols] = high
+        dhl_ref[1, at, cols] = (value - high.astype(jnp.float32)).astype(jnp.bfloat16)
+
+    def place(a, b, k, total):
+        if a + b > 0:
+            z_copy(a, k, b).wait_recv()
+        cols = pl.ds(k * LANES, LANES)
+        source = source_of(a, b)
+        rows = rows_in(a, b, k)
+        for r in range(groups - 1):
+            value = rows(r)
+            total = total + value
+            if r == 0:
+                edge_ref[source, 0, :, cols] = value
+            elif r == groups - 2:
+                edge_ref[source, 1, :, cols] = value
+            else:
+                put_halves(source * col_count + r * 16, cols, value)
+        return total
+
+    def finish_rims(k, total):
+        cols = pl.ds(k * LANES, LANES)
+        for a, b in moves + [(0, 0)]:
+            source = source_of(a, b)
+            after = (source + 1) % py_count
+            before = (source + py_count - 1) % py_count
+            rim = rows_in(a, b, k)(groups - 1)
+            first = jnp.where(row8 < 4, rim[:8], 0.0)
+            second = jnp.where(row8 > 4, rim[8:], 0.0)
+            edge_ref[after, 0, pl.ds(0, 8), cols] += first
+            edge_ref[before, 1, pl.ds(8, 8), cols] += second
+            total = total + jnp.concatenate([first, second], axis=0)
+        for source in range(py_count):
+            put_halves(source * col_count, cols, edge_ref[source, 0, :, cols])
+            put_halves((source + 1) * col_count - 16, cols, edge_ref[source, 1, :, cols])
+        return total
+
+    lead = min(5, chunks)
+    for c in range(lead):
+        add_pair(c)
+    gather(0)
+    for c in range(lead, chunks):
+        add_pair(c)
     total = jnp.zeros((16, LANES), jnp.float32)
-    for m in range(py_count - 1, -1, -1):
-        for s in range(chips - 1, 0, -1):
-            code_copy(m, s).wait_recv()
-
-        def gather(t, total):
-            scales = [
-                jnp.exp2(got_ref[m, s, t, pl.ds(col_count, 16), :].astype(jnp.int32)[8:9].astype(jnp.float32) - 15.0)
-                for s in range(1, chips)
+    waiting = [(a, b, k) for a in range(near - 1, 0, -1) for k in range(part) for b in (1, 0)]
+    for c in range(1, chunks):
+        if c == min(3, chunks - 1):
+            make_tables()
+        gather(c)
+        if c >= chunks - part:
+            for _ in range(2):
+                if waiting:
+                    total = place(*waiting.pop(0), total)
+    for k in range(part):
+        total = place(0, 0, k, total)
+    for a, b, k in waiting:
+        total = place(a, b, k, total)
+    for k in range(part):
+        total = place(0, 1, k, total)
+        total = finish_rims(k, total)
+    total = jnp.sum(total)
+    bucket_count = counts_ref.shape[1]
+    info_ref[...] = jnp.where(row8 == 0, total, 0.0)
+    info_ref[pl.ds(1, 1), pl.ds(0, bucket_count)] = counts_ref[...].astype(jnp.float32)
+    for s, e, a in others:
+        i_copy(s, e, a).start()
+
+    span = near * ky_part
+
+    def transform(s):
+        def stack(cos_ref, sin_ref):
+            rows = [
+                pl.ds(pl.multiple_of((((chip + s) % chips * 2 + v) * py_count + half * near) * ky_part, span), span)
+                for v in range(2)
             ]
-
-            for r in range(groups):
-                at = pl.ds(r * 16, 16)
-                value = own_ref[m, t, at, :]
-                for s in range(1, chips):
-                    term = got_ref[m, s, t, at, :].astype(jnp.int32).astype(jnp.float32) * scales[s - 1]
-                    if r == groups - 1:
-                        term = jnp.where(row16 == spare, 0.0, term)
-                    value = value + term
-                own_ref[m, t, at, :] = value
-                total = total + value
-            if m > 0:
-                def keep(r, value):
-                    zcode_ref[m, t, pl.ds(r * 16, 16), :] = value
-
-                code_block(lambda r: own_ref[m, t, pl.ds(r * 16, 16), :], keep, groups, spare)
-            return total
-
-        total = lax.fori_loop(0, part, gather, total)
-        if m > 0:
-            z_copy(m).start()
-
-    total = jnp.sum(total)
-
-    def place(m, reader):
-        source = (py + py_count - m) % py_count
-        for t in range(part):
-            cols = pl.ds(t * LANES, LANES)
-            for r in range(groups - 1):
-                data_ref[source, pl.ds(r * 16, 16), cols] = reader(t, r)
-
-    def rims(m, reader):
-        source = (py + py_count - m) % py_count
-        after = (source + 1) % py_count
-        before = (source + py_count - 1) % py_count
-        for t in range(part):
-            cols = pl.ds(t * LANES, LANES)
-            rim = reader(t, groups - 1)
-            low = pl.ds(0, 8)
-            high = pl.ds(col_count - 8, 8)
-            row = lax.broadcasted_iota(jnp.int32, (8, LANES), 0)
-            data_ref[after, low, cols] += jnp.where(row < 4, rim[:8], 0.0)
-            data_ref[before, high, cols] += jnp.where(row > 4, rim[8:], 0.0)
-
-    def own_reader(t, r):
-        return own_ref[0, t, pl.ds(r * 16, 16), :]
-
-    def z_reader(m):
-        def read(t, r):
-            scale = jnp.exp2(zgot_ref[m, t, pl.ds(col_count, 16), :].astype(jnp.int32)[8:9].astype(jnp.float32) - 15.0)
-            return zgot_ref[m, t, pl.ds(r * 16, 16), :].astype(jnp.int32).astype(jnp.float32) * scale
-        return read
-
-    readers = [own_reader] + [z_reader(m) for m in range(1, py_count)]
-    place(0, readers[0])
-    for m in range(py_count - 1, 0, -1):
-        z_copy(m).wait_recv()
-        place(m, readers[m])
-    for m in range(py_count):
-        rims(m, readers[m])
-    for j in range(py_count):
-        def halves(r, _):
-            at = pl.ds(pl.multiple_of(r * 16, 16), 16)
-            value = data_ref[j, at, :]
-            high = value.astype(jnp.bfloat16)
-            to = pl.ds(pl.multiple_of(j * col_count + r * 16, 16), 16)
-            dhl_ref[0, to, :] = high
-            dhl_ref[1, to, :] = (value - high.astype(jnp.float32)).astype(jnp.bfloat16)
-            return 0
-
-        lax.fori_loop(0, col_count // 16, halves, 0)
-
-    power = code_power(total)
-    scaled = total * jnp.exp2(14.0 - power)
-    first = jnp.clip(jnp.floor(scaled), 0.0, 32767.0)
-    second = jnp.clip(jnp.floor((scaled - first) * 16384.0), 0.0, 16384.0)
-    row8 = lax.broadcasted_iota(jnp.int32, (8, width), 0)
-    lane8 = lax.broadcasted_iota(jnp.int32, (8, width), 1)
-    number = jnp.where(lane8 == 0, power, jnp.where(lane8 == 1, first, second))
-    bucket_count = counts_ref.shape[1]
-    side_ref[...] = jnp.where(row8 == 1, number, 0.0)
-    side_ref[pl.ds(2, 1), pl.ds(0, bucket_count)] = counts_ref[...].astype(jnp.float32)
-    side = side_ref[...]
-    span = 2 * py_count * ky_part
-
-    def transform(s):
-        at = pl.ds(pl.multiple_of((chip + s) % chips * span, span), span)
-        for high_ref, low_ref, k in ((chi_ref, clo_ref, 0), (shi_ref, slo_ref, 1)):
-            value = jnp.dot(high_ref[at, :], dhl_ref[0], preferred_element_type=jnp.float32)
-            value += jnp.dot(high_ref[at, :], dhl_ref[1], preferred_element_type=jnp.float32)
-            value += jnp.dot(low_ref[at, :], dhl_ref[0], preferred_element_type=jnp.float32)
-            line_ref[k] = value if k == 0 else -value
+            return jnp.concatenate([ref[at, :] for ref in (cos_ref, sin_ref) for at in rows], axis=0)
+
+        high = stack(chi_ref, shi_ref)
+        low = stack(clo_ref, slo_ref)
+        for n in range(0, width, 256):
+            cols = pl.ds(n, 256)
+            both = jnp.dot(jnp.concatenate([high, low], axis=0), dhl_ref[0, :, cols],
+                           preferred_element_type=jnp.float32)
+            rest = jnp.dot(high, dhl_ref[1, :, cols], preferred_element_type=jnp.float32)
+            line_ref[:, cols] = both[: 4 * span] + both[4 * span :] + rest
+        row = lax.broadcasted_iota(jnp.int32, (8, width), 0)
         for e in range(2):
-            for m in range(py_count):
-                index = (core + e) % 2 * py_count + (py + m) % py_count
-                rows = pl.ds(pl.multiple_of(index * ky_part, ky_part), ky_part)
-                real = line_ref[0, rows, :]
-                imag = line_ref[1, rows, :]
+            for a in range(near):
+                at = (core + e) % 2 * span + (seat + a) % near * ky_part
+                real = line_ref[pl.ds(pl.multiple_of(at, ky_part), ky_part), :]
+                imag = -line_ref[pl.ds(pl.multiple_of(2 * span + at, ky_part), ky_part), :]
                 top = jnp.maximum(jnp.abs(real), jnp.abs(imag))
                 power = code_power(jnp.max(top, axis=0, keepdims=True))
                 factor = jnp.exp2(15.0 - power)
                 for k, value in enumerate((real, imag)):
                     steps = jnp.clip(jnp.round(value * factor), -32767.0, 32767.0)
-                    fcode_ref[s, e, m, pl.ds(k * ky_part, ky_part), :] = steps.astype(jnp.int32).astype(jnp.int16)
-                rest = jnp.where(row8 == 0, power, side)
-                fcode_ref[s, e, m, pl.ds(2 * ky_part, 8), :] = rest.astype(jnp.int32).astype(jnp.int16)
-
-    def send_all(s):
+                    fcode_ref[s, e, a, pl.ds(k * ky_part, ky_part), :] = steps.astype(jnp.int32).astype(jnp.int16)
+                rest = jnp.where(row == 0, power, 0.0)
+                fcode_ref[s, e, a, pl.ds(2 * ky_part, 8), :] = rest.astype(jnp.int32).astype(jnp.int16)
+
+    for s in SENDS:
         transform(s)
-        for e in range(2):
-            for m in range(py_count - 1, -1, -1):
-                f_copy(s, e, m).start()
-        return 0
-
-    lax.fori_loop(0, chips - 1, lambda k, _: send_all(chips - 1 - k), 0)
-    transform(0)
-    for e in range(1, -1, -1):
-        for m in range(py_count - 1, -1, -1):
-            if e + m > 0:
-                f_copy(0, e, m).start()
-
-    sum_total = total
-    column = jnp.zeros((8, width), jnp.float32)
-    before = jnp.zeros((8, width), jnp.float32)
+        for a in range(near - 1, -1, -1):
+            for e in range(1, -1, -1):
+                if s + e + a > 0:
+                    f_copy(s, e, a).start()
+
     rows_all = px_count * ky_part
-    for m in range(py_count):
-        source = (py + py_count - m) % py_count
-        for s in range(chips):
+    quarter = 2 * ky_part
+
+    def decode(s, e, a, ref):
+        scale = jnp.exp2(plain(ref[s, e, a, pl.ds(2 * ky_part, 8), :])[0:1] - 15.0)
+        cols = pl.ds(pl.multiple_of((seat + near - a) % near * width, width), width)
+        for k in range(2):
+            value = plain(ref[s, e, a, pl.ds(k * ky_part, ky_part), :]) * scale
+            high = value.astype(jnp.bfloat16)
+            at = k * quarter + e * ky_part
+            lhs_ref[pl.ds(at, ky_part), cols] = high
+            lhs_ref[pl.ds(2 * quarter + at, ky_part), cols] = (value - high.astype(jnp.float32)).astype(jnp.bfloat16)
+
+    def finish(s):
+        def some(n, _):
+            cols = pl.ds(pl.multiple_of(n * WIDE, WIDE), WIDE)
+            results = []
+            for high_ref, low_ref in ((chi_ref, clo_ref), (shi_ref, slo_ref)):
+                both = jnp.dot(lhs_ref[...], high_ref[:, cols], preferred_element_type=jnp.float32)
+                rest = jnp.dot(lhs_ref[pl.ds(0, 2 * quarter), :], low_ref[:, cols], preferred_element_type=jnp.float32)
+                results.append(both[: 2 * quarter] + both[2 * quarter :] + rest)
+            by_cos, by_sin = results
+            real = by_cos[:quarter] + by_sin[quarter:]
+            imag = by_cos[quarter:] - by_sin[:quarter]
             for e in range(2):
-                mine = m + s + e == 0
-                if not mine:
-                    f_copy(s, e, m).wait_recv()
-                got = fcode_ref if mine else fgot_ref
-                where = (0, 0, 0) if mine else (m, s, e)
                 sender = (chip + chips - s) % chips * 2 + (core + e) % 2
-                rest = got[where + (pl.ds(2 * ky_part, 8), slice(None))].astype(jnp.int32)
-                scale = jnp.exp2(rest[0:1].astype(jnp.float32) - 15.0)
-                info = rest.astype(jnp.float32)
-                if not mine:
-                    digit = info[1:2, :LANES]
-                    lane1 = lax.broadcasted_iota(jnp.int32, (1, LANES), 1)
-                    body = jnp.sum(jnp.where(lane1 == 1, digit, 0.0) + jnp.where(lane1 == 2, digit * (1.0 / 16384.0), 0.0))
-                    bits = jnp.sum(jnp.where(lane1 == 0, digit, 0.0))
-                    sum_total = sum_total + body * jnp.exp2(bits - 14.0)
-                if m == 0:
-                    column = column + info
-                    before = before + jnp.where(sender < px, info, 0.0)
-                rows = pl.ds(pl.multiple_of(sender * ky_part, ky_part), ky_part)
-                rows2 = pl.ds(pl.multiple_of(rows_all + sender * ky_part, ky_part), ky_part)
-                real = got[where + (pl.ds(0, ky_part), slice(None))].astype(jnp.int32).astype(jnp.float32) * scale
-                imag = got[where + (pl.ds(ky_part, ky_part), slice(None))].astype(jnp.int32).astype(jnp.float32) * scale
-                for at, a, b in ((rows, real, imag), (rows2, imag, -real)):
-                    for k, value in enumerate((a, b)):
-                        high = value.astype(jnp.bfloat16)
-                        lhs_ref[0, at, pl.ds(k * width, width)] = high
-                        lhs_ref[1, at, pl.ds(k * width, width)] = (value - high.astype(jnp.float32)).astype(jnp.bfloat16)
-
-        norm = 1.0 / math.sqrt(NX * NY)
-        factor = (PLANES * NX * NY * norm) / jnp.full((1, 256), sum_total, jnp.float32)
-        xrows = pl.ds(pl.multiple_of(source * width, width), width)
-
-        def columns(n, _):
-            cols = pl.ds(pl.multiple_of(n * 256, 256), 256)
-            high = lhs_ref[0]
-            low = lhs_ref[1]
-            ch, cl, sh, sl = (ref[xrows, cols] for ref in (chi_ref, clo_ref, shi_ref, slo_ref))
-            hh = jnp.concatenate([ch, sh], axis=0)
-            ll = jnp.concatenate([cl, sl], axis=0)
-            value = jnp.dot(high, hh, preferred_element_type=jnp.float32)
-            value += jnp.dot(low, hh, preferred_element_type=jnp.float32)
-            value += jnp.dot(high, ll, preferred_element_type=jnp.float32)
-            if m > 0:
-                value += out_ref[:, cols]
-            if m == py_count - 1:
-                value = value * factor
-            out_ref[:, cols] = value
+                at = pl.multiple_of(sender * ky_part, ky_part)
+                out_ref[pl.ds(at, ky_part), cols] = real[e * ky_part : (e + 1) * ky_part]
+                out_ref[pl.ds(rows_all + at, ky_part), cols] = imag[e * ky_part : (e + 1) * ky_part]
             return 0
 
-        lax.fori_loop(0, NX // 256, columns, 0)
-
-    first8 = lax.broadcasted_iota(jnp.int32, (8, LANES), 0) == 0
-    corner = first8 & (lax.broadcasted_iota(jnp.int32, (8, LANES), 1) + px + py == 0)
-    for plane in range(px_count):
-        at = pl.ds(plane * ky_part, 8)
-        out_ref[at, pl.ds(0, LANES)] -= jnp.where(corner, NX * NY * norm, 0.0)
-    sums = column[2:3]
-    lane = lax.broadcasted_iota(jnp.int32, (1, width), 1)
-    preceding = sums
+        lax.fori_loop(0, NX // WIDE, some, 0)
+
+    for s in TAKES:
+        for a in range(near):
+            for e in range(2):
+                if s + e + a == 0:
+                    decode(s, e, a, fcode_ref)
+                else:
+                    f_copy(s, e, a).wait_recv()
+                    decode(s, e, a, fgot_ref)
+        finish(s)
+
+    column = info_ref[pl.ds(1, 1), :]
+    before = jnp.zeros((1, LANES), jnp.float32)
+    sums = info_ref[...]
+    for s, e, a in others:
+        i_copy(s, e, a).wait_recv()
+        info = infos_ref[s, e, a]
+        sums = sums + info
+        if a == 0:
+            sender = (chip + chips - s) % chips * 2 + (core + e) % 2
+            column = column + info[1:2]
+            before = before + jnp.where(sender < px, info[1:2], 0.0)
+    lane = lax.broadcasted_iota(jnp.int32, (1, LANES), 1)
+    preceding = column
     step = 1
-    while step < width:
+    while step < LANES:
         preceding = preceding + jnp.where(lane >= step, pltpu.roll(preceding, step, 1), 0.0)
         step *= 2
-    begin = (preceding - sums + before[2:3]).astype(jnp.int32)
+    begin = (preceding - column + before).astype(jnp.int32)
     starts_ref[0] = begin[:, :bucket_count]
-
-    for m, s in order:
-        pair_copy(m, s).wait_send()
-        if s > 0:
-            code_copy(m, s).wait_send()
-    for m in range(1, py_count):
-        z_copy(m).wait_send()
-    for s in range(chips):
-        for e in range(2):
-            for m in range(py_count):
-                if s + e + m > 0:
-                    f_copy(s, e, m).wait_send()
+    total = jnp.broadcast_to(sums[0:1, 0:1], (1, NX))
+    factor_ref[0, 0] = (PLANES * NX * NY * norm) / total
+
+    corner = (row8 == 0) & (lax.broadcasted_iota(jnp.int32, (8, LANES), 1) + px + py == 0)
+    for plane in range(px_count):
+        out_ref[pl.ds(plane * ky_part, 8), pl.ds(0, LANES)] -= jnp.where(corner, total[:, :LANES] / PLANES, 0.0)
+
+    for c in range(chunks):
+        for s in range(chips):
+            pair_copy(c, s).wait_send()
+            if s > 0:
+                code_copy(c, s).wait_send()
+    for a, b in moves:
+        for k in range(part):
+            z_copy(a, k, b).wait_send()
+    for s, e, a in others:
+        f_copy(s, e, a).wait_send()
+        i_copy(s, e, a).wait_send()
 
 
 def exchange(grid, counts, tables, px_count, py_count):
     blocks, tiles, height, _ = grid.shape
     chips = px_count // 2
-    part = tiles // py_count
+    near = py_count // 2
+    part = tiles // near
+    chunks = near * part
     width = part * LANES
     col_count = height - 16
     ky_part = NY // (px_count * py_count)
-    span = 2 * py_count * ky_part
     rows = px_count * ky_part
     vmem = pl.BlockSpec(memory_space=pltpu.VMEM)
     dma = pltpu.SemaphoreType.DMA
@@ -691,36 +731,40 @@
         out_shape=(
             jax.ShapeDtypeStruct((2 * rows, NX), f32),
             jax.ShapeDtypeStruct((1,) + counts.shape, jnp.int32),
+            jax.ShapeDtypeStruct((1, 1, 1, NX), f32),
         ),
         in_specs=[vmem] * 2 + [pl.BlockSpec(memory_space=pltpu.HBM)] * 4,
-        out_specs=[vmem] * 2,
+        out_specs=[vmem] * 3,
         scratch_shapes=[pltpu.VMEM((32, NX), f32)] * 4
         + [
-            pltpu.VMEM((8, width), f32),
             dma((4,)),
-            pltpu.VMEM((py_count, chips, part, height, LANES), f32),
-            pltpu.VMEM((py_count, part, height, LANES), f32),
-            pltpu.VMEM((py_count, chips, part, height, LANES), s16),
-            pltpu.VMEM((py_count, chips, part, height, LANES), s16),
-            pltpu.VMEM((py_count, part, height, LANES), s16),
-            pltpu.VMEM((py_count, part, height, LANES), s16),
-            pltpu.VMEM((py_count, col_count, width), f32),
+            pltpu.VMEM((chunks, chips, height, LANES), f32),
+            pltpu.VMEM((chunks, height, LANES), f32),
+            pltpu.VMEM((chunks, chips - 1, height, LANES), s16),
+            pltpu.VMEM((chunks, chips - 1, height, LANES), s16),
+            pltpu.VMEM((near, part, height, LANES), s16),
+            pltpu.VMEM((near, 2, part, height, LANES), s16),
+            pltpu.VMEM((py_count, 2, 16, width), f32),
             pltpu.VMEM((2, NY, width), bf16),
         ]
         + [pltpu.VMEM((NX, NX), bf16)] * 4
         + [
-            pltpu.VMEM((chips, 2, py_count, 2 * ky_part + 8, width), s16),
-            pltpu.VMEM((py_count, chips, 2, 2 * ky_part + 8, width), s16),
-            pltpu.VMEM((2, 2 * rows, 2 * width), bf16),
-            pltpu.VMEM((2, span, width), f32),
-            dma((py_count, chips)),
-            dma((py_count, chips)),
-            dma((py_count, chips)),
-            dma((py_count, chips)),
-            dma((py_count,)),
-            dma((py_count,)),
-            dma((chips, 2, py_count)),
-            dma((chips, 2, py_count)),
+            pltpu.VMEM((chips, 2, near, 2 * ky_part + 8, width), s16),
+            pltpu.VMEM((chips, 2, near, 2 * ky_part + 8, width), s16),
+            pltpu.VMEM((8 * ky_part, NX), bf16),
+            pltpu.VMEM((4 * near * ky_part, width), f32),
+            pltpu.VMEM((8, LANES), f32),
+            pltpu.VMEM((chips, 2, near, 8, LANES), f32),
+            dma((chunks, chips)),
+            dma((chunks, chips)),
+            dma((chunks, chips - 1)),
+            dma((chunks, chips - 1)),
+            dma((near, 2, part)),
+            dma((near, 2, part)),
+            dma((chips, 2, near)),
+            dma((chips, 2, near)),
+            dma((chips, 2, near)),
+            dma((chips, 2, near)),
         ],
         compiler_params=pltpu.CompilerParams(
             collective_id=0, has_side_effects=True, vmem_limit_bytes=EXCHANGE_VMEM * 1024 * 1024
@@ -743,9 +787,9 @@
     )
     bucket_count = counts.shape[-1]
     lane_tiles = NX // LANES
-    if px_count == PLANES and lane_tiles % py_count == 0 and bucket_count <= LANES:
-        out, begin = exchange(grid, counts[0], dft_parts(), px_count, py_count)
-        return (out.reshape(2, PLANES, ky_part, NX), begin)
+    if px_count == PLANES and py_count % 2 == 0 and lane_tiles % py_count == 0 and bucket_count <= LANES:
+        out, begin, factor = exchange(grid, counts[0], dft_parts(), px_count, py_count)
+        return (out.reshape(2, PLANES, ky_part, NX) * factor, begin)
     grid = grid.transpose(0, 2, 1, 3).reshape(PLANES, col_count + 16, NX)
     height = col_count + 16
     width = NX // parts

time: 103 us -> 93 us (0.903); the launches traced: 103 us -> 94.3 us
  Pallas kernels: 100 us -> 91.5 us
  other arithmetic: 0 us -> 1.57 us
  local copies, waits for them, and re-layouts: 1.86 us -> 0.54 us
    pallas_call x1, Pallas kernels: 73.7 us -> 64.8 us  [exchange(): pl.pallas_call(functools.partial(exchange_kernel, px_count, py_count), ou...]
    mul x0 -> x1, other arithmetic: none -> 1.57 us  [local(): return (out.reshape(2, PLANES, ky_part, NX) * factor, begin)]
    unnamed x12 -> x11, local copies, waits for them, and re-layouts: 1.86 us -> 0.54 us
where the time goes in v3:
time: 93 us; the launch traced here: 94.3 us
  Pallas kernels  91.5 us (98%)
  other arithmetic  1.57 us (2%)
    pallas_call x1, Pallas kernels, exchange(): pl.pallas_call(functools.partial(exchange_kernel, px_count, py_count), ou...  64.8 us
    pallas_call x1, Pallas kernels, spread(): pl.pallas_call(functools.partial(spread_kernel, row_count, col_count, buc...  26.7 us

profile of v3, /device:TPU:16, one launch (start us, length us, event | category | flops | bytes accessed | tf_op | source)
XLA Modules:
  0.0 94.3 jit_solution(1903819774512896719)
XLA Ops:
  0.6 0.0 copy-start
  0.6 0.0 copy-start.1
  0.7 0.0 copy-start.2
  0.7 0.0 copy-start.3
  0.7 0.0 copy-start.4
  0.7 26.7 %spread.1.grid_ref = f32[8,8,272,128]{3,2,1,0:T(8,128)S(1)} custom-call(s32[640,128]{1,0:T(8,128)} %bitcast.11, s32[1,640]{1,0:T(1,128)} %owner_in.1, bf16[640,128]{1,0:T(8,128)(2,1)} %bitcast.13, bf16[640,128]{1,0:T(8,128)(2,1)} %bitcast.14, bf16[640,128]{1,0:T(8,128)(2,1)} %bitcast.15, s32[640,128]{1,0:T(8,128)} %bitcast.12), custom_call_target="tpu_custom_call" | custom-call | tf_op jit(solution)/shard_map/spread/pallas_call | solution.py:195
  27.4 0.0 copy-done
  27.4 0.0 copy-done.1
  27.5 0.0 copy-done.2
  27.5 0.0 copy-done.3
  27.5 0.0 copy-done.4
  27.5 64.8 %exchange.1 = (f32[512,1024]{1,0:T(8,128)S(1)}, s32[1,1,64]{2,1,0:T(1,128)S(1)}, f32[1,1,1,1024]{3,2,1,0:T(1,128)S(1)}) custom-call(f32[8,8,272,128]{3,2,1,0:T(8,128)S(1)} %spread.1.grid_ref, s32[1,64]{1,0:T(1,128)S(1)} %bitcast.10, f32[32,1024]{1,0:T(8,128)S(1)} %copy-done.3, f32[32,1024]{1,0:T(8,128)S(1)} %copy-done.2, f32[32,1024]{1,0:T(8,128)S(1)} %copy-done.1, ...), custom_call_target="tpu_custom_call" | custom-call | tf_op jit(solution)/shard_map/exchange/pallas_call | solution.py:729
  92.2 1.6 %broadcast_multiply_fusion = f32[2,8,32,1024]{3,2,1,0:T(8,128)} fusion(f32[2,8,32,1024]{3,2,1,0:T(8,128)S(1)} %bitcast.8, f32[1024]{0:T(1024)S(1)} %bitcast.9), kind=kLoop, calls=%fused_computation | loop fusion | flops 524288 | bytes 4198400 | tf_op jit(solution)/shard_map/mul | solution.py:792
  93.8 0.5 copy.14
Async XLA Ops:
  0.6 26.8 %copy-start = (f32[32,1024]{1,0:T(8,128)S(1)}, f32[32,1024]{1,0:T(8,128)}, u32[]{:S(2)}) copy-start(f32[32,1024]{1,0:T(8,128)} %constant.12.clone.fine_s_in) | copy-start | bytes 393220
  0.6 26.8 %copy-start.1 = (f32[32,1024]{1,0:T(8,128)S(1)}, f32[32,1024]{1,0:T(8,128)}, u32[]{:S(2)}) copy-start(f32[32,1024]{1,0:T(8,128)} %constant.11.clone.fine_c_in) | copy-start | bytes 393220
  0.7 26.8 %copy-start.2 = (f32[32,1024]{1,0:T(8,128)S(1)}, f32[32,1024]{1,0:T(8,128)}, u32[]{:S(2)}) copy-start(f32[32,1024]{1,0:T(8,128)} %constant.10.clone.coarse_s_in) | copy-start | bytes 393220
  0.7 26.8 %copy-start.3 = (f32[32,1024]{1,0:T(8,128)S(1)}, f32[32,1024]{1,0:T(8,128)}, u32[]{:S(2)}) copy-start(f32[32,1024]{1,0:T(8,128)} %constant.4.clone.coarse_c_in) | copy-start | bytes 393220
  0.7 26.8 %copy-start.4 = (s32[1,1,64]{2,1,0:T(1,128)S(1)}, s32[1,1,64]{2,1,0:T(1,128)}, u32[]{:S(2)}) copy-start(s32[1,1,64]{2,1,0:T(1,128)} %param.17) | copy-start | bytes 772

commit v4 on v3

--- a/solution.py
+++ b/solution.py
@@ -125,7 +125,7 @@
 
         return at + count
 
-    items = lax.fori_loop(0, bucket_count, of_bucket, 0)
+    items = lax.fori_loop(0, bucket_count, of_bucket, 0, unroll=4)
     for k in range(UNROLL):
         item_ref[items + k] = (bucket_count - 1) * 65536 + tiles
 
@@ -169,9 +169,8 @@
     lane = lax.broadcasted_iota(jnp.int32, (8, LANES), 1)
 
     def close(i, _):
-        plane = i // 2
-        for k in range(lane_tiles // 2):
-            tile = i % 2 * (lane_tiles // 2) + k
+        plane = i
+        for tile in range(lane_tiles):
             low = (tile + lane_tiles - 1) % lane_tiles
             high = (tile + 1) % lane_tiles
             for r in range(0, height, 8):
@@ -181,7 +180,7 @@
                 out_ref[plane, tile, at, :] += left + pltpu.roll(right, LANES - 16, 1)
         return 0
 
-    lax.fori_loop(0, 2 * PLANES, close, 0)
+    lax.fori_loop(0, PLANES, close, 0)
 
 
 def spread(cells, owners, fx, fy, mass, live, row_count, col_count, bucket_count):

time: 93 us -> 93.3 us (level)
  the two profiles are of different devices: /device:TPU:16 before, /device:TPU:10 now
where the time goes in v4:
time: 93.3 us; the launch traced here: 92.2 us
  Pallas kernels  89.3 us (96%)
  other arithmetic  1.57 us (2%)
    pallas_call x1, Pallas kernels, exchange(): pl.pallas_call(functools.partial(exchange_kernel, px_count, py_count), ou...  63.4 us
    pallas_call x1, Pallas kernels, spread(): pl.pallas_call(functools.partial(spread_kernel, row_count, col_count, buc...  25.9 us

profile of v4, /device:TPU:10, one launch (start us, length us, event | category | flops | bytes accessed | tf_op | source)
XLA Modules:
  0.0 92.2 jit_solution(11668374994089779329)
XLA Ops:
  0.6 0.0 copy-start
  0.6 0.0 copy-start.1
  0.7 0.0 copy-start.2
  0.7 0.0 copy-start.3
  0.7 0.0 copy-start.4
  0.7 25.9 %spread.1.grid_ref = f32[8,8,272,128]{3,2,1,0:T(8,128)S(1)} custom-call(s32[640,128]{1,0:T(8,128)} %bitcast.11, s32[1,640]{1,0:T(1,128)} %owner_in.1, bf16[640,128]{1,0:T(8,128)(2,1)} %bitcast.13, bf16[640,128]{1,0:T(8,128)(2,1)} %bitcast.14, bf16[640,128]{1,0:T(8,128)(2,1)} %bitcast.15, s32[640,128]{1,0:T(8,128)} %bitcast.12), custom_call_target="tpu_custom_call" | custom-call | tf_op jit(solution)/shard_map/spread/pallas_call | solution.py:194
  26.6 0.0 copy-done
  26.6 0.0 copy-done.1
  26.6 0.0 copy-done.2
  26.7 0.0 copy-done.3
  26.7 0.0 copy-done.4
  26.7 63.4 %exchange.1 = (f32[512,1024]{1,0:T(8,128)S(1)}, s32[1,1,64]{2,1,0:T(1,128)S(1)}, f32[1,1,1,1024]{3,2,1,0:T(1,128)S(1)}) custom-call(f32[8,8,272,128]{3,2,1,0:T(8,128)S(1)} %spread.1.grid_ref, s32[1,64]{1,0:T(1,128)S(1)} %bitcast.10, f32[32,1024]{1,0:T(8,128)S(1)} %copy-done.3, f32[32,1024]{1,0:T(8,128)S(1)} %copy-done.2, f32[32,1024]{1,0:T(8,128)S(1)} %copy-done.1, ...), custom_call_target="tpu_custom_call" | custom-call | tf_op jit(solution)/shard_map/exchange/pallas_call | solution.py:728
  90.1 1.6 %broadcast_multiply_fusion = f32[2,8,32,1024]{3,2,1,0:T(8,128)} fusion(f32[2,8,32,1024]{3,2,1,0:T(8,128)S(1)} %bitcast.8, f32[1024]{0:T(1024)S(1)} %bitcast.9), kind=kLoop, calls=%fused_computation | loop fusion | flops 524288 | bytes 4198400 | tf_op jit(solution)/shard_map/mul | solution.py:791
  91.7 0.5 copy.14
Async XLA Ops:
  0.6 26.0 %copy-start = (f32[32,1024]{1,0:T(8,128)S(1)}, f32[32,1024]{1,0:T(8,128)}, u32[]{:S(2)}) copy-start(f32[32,1024]{1,0:T(8,128)} %constant.12.clone.fine_s_in) | copy-start | bytes 393220
  0.6 26.0 %copy-start.1 = (f32[32,1024]{1,0:T(8,128)S(1)}, f32[32,1024]{1,0:T(8,128)}, u32[]{:S(2)}) copy-start(f32[32,1024]{1,0:T(8,128)} %constant.11.clone.fine_c_in) | copy-start | bytes 393220
  0.7 26.0 %copy-start.2 = (f32[32,1024]{1,0:T(8,128)S(1)}, f32[32,1024]{1,0:T(8,128)}, u32[]{:S(2)}) copy-start(f32[32,1024]{1,0:T(8,128)} %constant.10.clone.coarse_s_in) | copy-start | bytes 393220
  0.7 26.0 %copy-start.3 = (f32[32,1024]{1,0:T(8,128)S(1)}, f32[32,1024]{1,0:T(8,128)}, u32[]{:S(2)}) copy-start(f32[32,1024]{1,0:T(8,128)} %constant.4.clone.coarse_c_in) | copy-start | bytes 393220
  0.7 26.0 %copy-start.4 = (s32[1,1,64]{2,1,0:T(1,128)S(1)}, s32[1,1,64]{2,1,0:T(1,128)}, u32[]{:S(2)}) copy-start(s32[1,1,64]{2,1,0:T(1,128)} %param.17) | copy-start | bytes 772
